TPU v7x, 256 devices: a whole 4x4x8 slice. The times are simulated.
256 devices in a mesh: hot: 64 (over z, y, x_lo), cold: 4 (over x_hi, core).
Axes of the slice: x: 4 (x_hi: 2, x_lo: 2; x = x_hi * 2 + x_lo), y: 4, z: 8, core: 2. Of those that a mesh axis runs over, the one named last changes fastest.
Arguments:
- tokens: bfloat16 [64, 8192], replicated, may hold values from -6 to 6
- norm_gain: float32 [8192], replicated, may hold values from 0.1 to 1.9
- hot_gate: bfloat16 [4096, 8192], P(('hot', 'cold')), may hold values from -0.0625 to 0.0625
- hot_up: bfloat16 [4096, 8192], P(('hot', 'cold')), may hold values from -0.0625 to 0.0625
- hot_down: bfloat16 [4096, 8192], P(('hot', 'cold')), may hold values from -0.21875 to 0.21875
- hot_index: int32 [4096], replicated, may hold values from 0 to 14335, as said below
- cold_gate: bfloat16 [8192, 14336], P('hot', 'cold'), may hold values from -0.0625 to 0.0625
- cold_up: bfloat16 [8192, 14336], P('hot', 'cold'), may hold values from -0.0625 to 0.0625
- cold_down: bfloat16 [14336, 8192], P('cold', 'hot'), may hold values from -0.125 to 0.125
- block_mask: int32 [64, 112], P(None, 'cold'), may hold values from 0 to 1, as said below
Outputs:
- ffn_out: bfloat16 [64, 8192], P(None, ('hot', 'cold'))
Inputs may be any that keep to these rules, and one draw needn't show every extreme that they name: `hot_index`: distinct hidden units. `block_mask`: in each run of 28 blocks held by one index of cold, at most 14 blocks are active for any sequence, and some index reaches exactly 14.
All inputs are finite; a program needn't handle non-finite values.
Results may differ from a plain program's by a relative error of at most 0.0065.
Values may be sent and summed in bfloat16 or wider, within the bound.
A program may use at most 64 MiB of HBM per device.

v0:
```python
import jax
import jax.numpy as jnp
from jax import lax
from jax.sharding import Mesh
from jax.sharding import PartitionSpec as P

UNITS = 14336
COLD = ("cold_0", "cold_1")
HOT = ("hot_0", "hot_1", "hot_2")
HOT_COLD = ("hot_0", "hot_1", "hot_2", "cold_0", "cold_1")


def copy_for_each(x, axis):
    devices = lax.axis_size(axis)
    return lax.all_to_all(jnp.broadcast_to(x[None], (devices, *x.shape)), axis, 0, 0, tiled=True)


def joined_along(pieces, dim):
    shape = list(pieces.shape[1:])
    shape[dim] *= pieces.shape[0]
    return jnp.moveaxis(pieces, 0, dim).reshape(shape)


def collect(x, axis, dim):
    pieces = copy_for_each(x, axis)
    return joined_along(pieces, dim)


def all_blocks(x, axes, sequence):
    pieces = x
    for k in sequence:
        pieces = lax.all_gather(pieces, axes[k])
    done = sequence[::-1]
    back = [done.index(k) for k in range(len(axes))]
    pieces = pieces.transpose(*back, *range(len(axes), pieces.ndim))
    return pieces.reshape(-1, *x.shape)


def gathered_by_axis(x, axes, sequence, dim):
    return joined_along(all_blocks(x, axes, sequence), dim)


def cut_along(x, dim, devices):
    before, after = (x.shape[:dim], x.shape[dim + 1 :])
    return jnp.moveaxis(x.reshape(*before, devices, -1, *after), dim, 0)


def summed_on_arrival(x, axis, dim):
    pieces = cut_along(x, dim, lax.axis_size(axis))
    arrived = lax.all_to_all(pieces, axis, split_axis=0, concat_axis=0, tiled=True)
    return arrived.sum(axis=0)


def on_device(
    tokens,
    norm_gain,
    hot_gate,
    hot_up,
    hot_down,
    hot_index,
    cold_gate,
    cold_up,
    cold_down,
    block_mask,
):
    values = tokens.astype(jnp.float32)
    scale = lax.rsqrt(jnp.mean(values * values, axis=1, keepdims=True) + 1e-05)
    normed = (values * scale * norm_gain[None, :]).astype(jnp.bfloat16)
    dims = (((1,), (1,)), ((), ()))
    gate_hot = lax.dot_general(normed, hot_gate, dims, preferred_element_type=jnp.float32)
    up_hot = lax.dot_general(normed, hot_up, dims, preferred_element_type=jnp.float32)
    hidden_hot = (jax.nn.silu(gate_hot) * up_hot).astype(jnp.bfloat16)
    feat_rows = cold_gate.shape[0]
    unit_count = cold_gate.shape[1]
    out_cols = cold_down.shape[1]
    blocks_here = block_mask.shape[1]
    block = unit_count // blocks_here
    seqs = tokens.shape[0]
    is_hot = jnp.zeros((UNITS,), jnp.float32).at[hot_index].set(1.0)
    local_hot = lax.dynamic_slice_in_dim(is_hot, lax.axis_index(COLD) * unit_count, unit_count)
    capacity = blocks_here // 2
    positions = jnp.arange(blocks_here, dtype=jnp.int32)
    active = jnp.max(block_mask, axis=0) > 0
    slots = jnp.argsort(jnp.where(active, positions, positions + blocks_here))[:capacity]
    gate_w = cold_gate.reshape(feat_rows, blocks_here, block)[:, slots].reshape(
        feat_rows, capacity * block
    )
    up_w = cold_up.reshape(feat_rows, blocks_here, block)[:, slots].reshape(
        feat_rows, capacity * block
    )
    down_w = cold_down.reshape(blocks_here, block, out_cols)[slots].reshape(
        capacity * block, out_cols
    )
    seq_live = block_mask[:, slots].astype(jnp.float32)
    unit_live = 1.0 - local_hot.reshape(blocks_here, block)[slots]
    live = (seq_live[:, :, None] * unit_live[None, :, :]).reshape(seqs, capacity * block)
    gate_cols, up_cols = (
        lax.all_to_all(gate_w, HOT, split_axis=1, concat_axis=0, tiled=True),
        lax.all_to_all(up_w, HOT, split_axis=1, concat_axis=0, tiled=True),
    )
    gate_share = jnp.dot(normed, gate_cols, preferred_element_type=jnp.float32)
    up_share = jnp.dot(normed, up_cols, preferred_element_type=jnp.float32)
    share = gate_share.shape[1]
    live_share = lax.dynamic_slice_in_dim(live, lax.axis_index(HOT) * share, share, 1)
    piece = (jax.nn.silu(gate_share) * up_share * live_share).astype(jnp.bfloat16)
    hidden_cold = collect(piece, HOT, 1)
    out_cold = jnp.dot(hidden_cold, down_w, preferred_element_type=jnp.float32)
    down_cols = lax.all_to_all(hot_down, HOT_COLD, split_axis=1, concat_axis=0, tiled=True)
    hidden_all = gathered_by_axis(
        hidden_hot, (("hot_0", "hot_1", "hot_2", "cold_0"), "cold_1"), (0, 1), 1
    )
    hot_total = jnp.dot(hidden_all, down_cols, preferred_element_type=jnp.float32)
    cold_total = summed_on_arrival(out_cold, COLD, 1)
    total = hot_total + cold_total
    return total.astype(jnp.bfloat16)


def solution(mesh):
    split = Mesh(
        mesh.devices.reshape(8, 4, 2, 2, 2), ("hot_0", "hot_1", "hot_2", "cold_0", "cold_1")
    )
    placed = (
        P(),
        P(),
        P(HOT_COLD, None),
        P(HOT_COLD, None),
        P(HOT_COLD, None),
        P(),
        P(HOT, COLD),
        P(HOT, COLD),
        P(COLD, HOT),
        P(None, COLD),
    )
    return jax.shard_map(
        on_device, mesh=split, in_specs=placed, out_specs=P(None, HOT_COLD), check_vma=False
    )
```

profile of v0, /device:TPU:1, one launch (start us, length us, event | category | flops | bytes accessed | tf_op | source)
XLA Modules:
  0.0 460.4 jit_solution(4958017223762994111)
XLA Ops:
  0.0 0.9 reduce_max.9
  0.9 1.6 sort.17
  2.6 1.6 copy.32
  4.1 0.6 copy.33
  4.8 0.6 gather_fusion
  5.7 0.9 all_to_all.49
  6.6 13.6 %all-to-all-start.1 = ((bf16[128,64,28]{0,2,1:T(8,128)(2,1)}), bf16[128,64,28]{0,2,1:T(8,128)(2,1)S(1)}, u32[]{:S(2)}, u32[]{:S(2)}) async-start(bf16[128,64,28]{0,2,1:T(8,128)(2,1)} %all_to_all.49), calls=%async_computation.1 | async-start | bytes 1048576 | tf_op jit(solution)/shard_map/all_to_all | solution.py:98
  20.2 0.6 copy.36
  20.8 0.6 copy.37
  21.5 0.6 gather_fusion.1
  22.4 0.9 all_to_all.53
  23.3 15.5 %scatter_custom_fusion = f32[14336]{0:T(1024)S(1)} fusion(s32[4096]{0:T(1024)S(1)} %compare_select_fusion, f32[4096]{0:T(1024)S(1)} %broadcast.41, f32[]{:T(128)} %constant.17.clone.1), kind=kCustom, calls=%fused_computation.27 | custom fusion | bytes 57348 | tf_op jit(solution)/shard_map/scatter | solution.py:79
  38.9 10.9 %all-to-all-start.2 = ((bf16[128,64,28]{0,2,1:T(8,128)(2,1)}), bf16[128,64,28]{0,2,1:T(8,128)(2,1)}, u32[]{:S(2)}, u32[]{:S(2)}) async-start(bf16[128,64,28]{0,2,1:T(8,128)(2,1)} %all_to_all.53), calls=%async_computation.2 | async-start | bytes 1048576 | tf_op jit(solution)/shard_map/all_to_all | solution.py:99
  51.0 0.8 all_to_all.46
  51.8 0.7 copy.51
  52.5 1.4 reshape.134
  54.9 9.8 %all-to-all-done.2 = bf16[128,64,28]{0,2,1:T(8,128)(2,1)} async-done(((bf16[128,64,28]{0,2,1:T(8,128)(2,1)}), bf16[128,64,28]{0,2,1:T(8,128)(2,1)}, u32[]{:S(2)}, u32[]{:S(2)}) %all-to-all-start.2) | async-done | bytes 458784 | tf_op jit(solution)/shard_map/all_to_all | solution.py:99
  64.7 1.2 copy.49
  67.8 1.0 reshape.130
  68.8 7.0 %all-to-all-start.3 = ((bf16[64,2,896]{2,1,0:T(2,128)(2,1)}), bf16[64,2,896]{2,1,0:T(2,128)(2,1)S(1)}, u32[]{:S(2)}, u32[]{:S(2)}) async-start(bf16[64,2,896]{2,1,0:T(2,128)(2,1)} %reshape.130), calls=%async_computation.3 | async-start | bytes 458752 | tf_op jit(solution)/shard_map/all_to_all | solution.py:15
  77.2 8.9 %all-to-all-done.3 = bf16[64,2,896]{2,1,0:T(2,128)(2,1)S(1)} async-done(((bf16[64,2,896]{2,1,0:T(2,128)(2,1)}), bf16[64,2,896]{2,1,0:T(2,128)(2,1)S(1)}, u32[]{:S(2)}, u32[]{:S(2)}) %all-to-all-start.3) | async-done | bytes 229408 | tf_op jit(solution)/shard_map/all_to_all | solution.py:15
  86.1 10.0 %all-to-all-start = ((bf16[256,2,256]{2,1,0:T(2,128)(2,1)}), bf16[256,2,256]{2,1,0:T(2,128)(2,1)S(1)}, u32[]{:S(2)}, u32[]{:S(2)}) async-start(bf16[256,2,256]{2,1,0:T(2,128)(2,1)} %reshape.134), calls=%async_computation | async-start | bytes 524288 | tf_op jit(solution)/shard_map/all_to_all | solution.py:108
  96.1 294.4 %all-gather.2 = bf16[128,64,16]{1,2,0:T(8,128)(2,1)S(1)} all-gather(bf16[1,64,16]{1,2,0:T(8,128)(2,1)S(1)} %fusion.8), channel_id=2, replica_groups=mesh['hot_0'=8,'hot_1'=4,'hot_2'=2,'cold_0'=2,'cold_1'=2] {'hot_0','hot_..., dimensions={0}, use_global_device_ids=true | all-gather | bytes 264192 | tf_op jit(solution)/shard_map/all_gather | solution.py:32
  390.5 0.8 gather_fusion.4
  392.9 0.7 reshape.132
  393.6 58.8 %all-to-all-start.4 = ((f32[4,1,2048]{2,1,0:T(1,128)}), f32[4,1,2048]{2,1,0:T(1,128)S(1)}, u32[]{:S(2)}, u32[]{:S(2)}) async-start(f32[4,1,2048]{2,1,0:T(1,128)} %reshape.132), calls=%async_computation.4 | async-start | bytes 65536 | tf_op jit(solution)/shard_map/all_to_all | solution.py:50
  452.4 2.2 all-gather.1
  454.8 1.2 copy.28
  456.0 0.8 copy.29
  457.4 0.8 copy.31
  458.7 0.7 reduce
  459.6 0.9 fusion.5
  (61 shorter events, 8.9 us)
Async XLA Ops:
  0.0 390.5 %copy-start = (bf16[3584,128]{1,0:T(8,128)(2,1)S(1)}, bf16[3584,128]{1,0:T(8,128)(2,1)}, u32[]{:S(2)}) copy-start(bf16[3584,128]{1,0:T(8,128)(2,1)} %param.18) | copy-start | bytes 2752516
  2.6 47.9 %copy-start.6 = (s32[1024]{0:T(1024)}, s32[1024]{0:T(1024)S(1)}, u32[]{:S(2)}) copy-start(s32[1024]{0:T(1024)S(1)} %pad_clamp_fusion) | copy-start | bytes 12292
  5.7 14.5 %copy-start.3 = (bf16[128,3584]{1,0:T(8,128)(2,1)S(1)}, bf16[128,3584]{1,0:T(8,128)(2,1)}, u32[]{:S(2)}) copy-start(bf16[128,3584]{1,0:T(8,128)(2,1)} %param.17) | copy-start | bytes 2752516
  6.6 32.3 %all-to-all-start.1 = ((bf16[128,64,28]{0,2,1:T(8,128)(2,1)}), bf16[128,64,28]{0,2,1:T(8,128)(2,1)S(1)}, u32[]{:S(2)}, u32[]{:S(2)}) async-start(bf16[128,64,28]{0,2,1:T(8,128)(2,1)} %all_to_all.49), calls=%async_computation.1 | async-start | bytes 1048576 | tf_op jit(solution)/shard_map/all_to_all | solution.py:98
  22.1 1.2 copy-start.5
  22.4 27.5 %copy-start.1 = (s32[64,28]{0,1:T(8,128)S(1)}, s32[64,28]{0,1:T(8,128)}, u32[]{:S(2)}) copy-start(s32[64,28]{0,1:T(8,128)} %param.19) | copy-start | bytes 21508
  22.4 28.6 %copy-start.4 = (bf16[16,8192]{1,0:T(8,128)(2,1)S(1)}, bf16[16,8192]{1,0:T(8,128)(2,1)}, u32[]{:S(2)}) copy-start(bf16[16,8192]{1,0:T(8,128)(2,1)} %param.14) | copy-start | bytes 786436
  38.9 25.9 %all-to-all-start.2 = ((bf16[128,64,28]{0,2,1:T(8,128)(2,1)}), bf16[128,64,28]{0,2,1:T(8,128)(2,1)}, u32[]{:S(2)}, u32[]{:S(2)}) async-start(bf16[128,64,28]{0,2,1:T(8,128)(2,1)} %all_to_all.53), calls=%async_computation.2 | async-start | bytes 1048576 | tf_op jit(solution)/shard_map/all_to_all | solution.py:99
  52.5 1.5 copy-start.2
  65.9 0.8 copy-start.9
  67.7 8.0 %copy-start.7 = (bf16[16,8192]{1,0:T(8,128)(2,1)S(1)}, bf16[16,8192]{1,0:T(8,128)(2,1)}, u32[]{:S(2)}) copy-start(bf16[16,8192]{1,0:T(8,128)(2,1)} %param.12) | copy-start | bytes 786436
  68.8 17.3 %all-to-all-start.3 = ((bf16[64,2,896]{2,1,0:T(2,128)(2,1)}), bf16[64,2,896]{2,1,0:T(2,128)(2,1)S(1)}, u32[]{:S(2)}, u32[]{:S(2)}) async-start(bf16[64,2,896]{2,1,0:T(2,128)(2,1)} %reshape.130), calls=%async_computation.3 | async-start | bytes 458752 | tf_op jit(solution)/shard_map/all_to_all | solution.py:15
  75.8 1.0 copy-start.8
  86.1 307.5 %all-to-all-start = ((bf16[256,2,256]{2,1,0:T(2,128)(2,1)}), bf16[256,2,256]{2,1,0:T(2,128)(2,1)S(1)}, u32[]{:S(2)}, u32[]{:S(2)}) async-start(bf16[256,2,256]{2,1,0:T(2,128)(2,1)} %reshape.134), calls=%async_computation | async-start | bytes 524288 | tf_op jit(solution)/shard_map/all_to_all | solution.py:108
  393.6 64.6 %all-to-all-start.4 = ((f32[4,1,2048]{2,1,0:T(1,128)}), f32[4,1,2048]{2,1,0:T(1,128)S(1)}, u32[]{:S(2)}, u32[]{:S(2)}) async-start(f32[4,1,2048]{2,1,0:T(1,128)} %reshape.132), calls=%async_computation.4 | async-start | bytes 65536 | tf_op jit(solution)/shard_map/all_to_all | solution.py:50
where the time goes:
time: 461 us; the launch traced here: 460 us
  blocking collectives  297 us (64%)
  starting transfers between devices  100 us (22%)
  local copies, waits for them, and re-layouts  37.9 us (8%)
  waiting for transfers between devices  18.7 us (4%)
    all_gather x2, blocking collectives, all_blocks(): pieces = lax.all_gather(pieces, axes[k])  297 us
    all_to_all x1, starting transfers between devices, summed_on_arrival(): lax.all_to_all(pieces, axis, split_axis=0, concat_axis=0, tiled=True)  58.8 us
    scatter x1, local copies, waits for them, and re-layouts, on_device(): is_hot = jnp.zeros((UNITS,), jnp.float32).at[hot_index].set(1.0)  15.5 us
    all_to_all x1, starting transfers between devices, on_device(): lax.all_to_all(gate_w, HOT, split_axis=1, concat_axis=0, tiled=True)  13.6 us
    all_to_all x1, starting transfers between devices, on_device(): lax.all_to_all(up_w, HOT, split_axis=1, concat_axis=0, tiled=True)  10.9 us
    all_to_all x1, starting transfers between devices, on_device(): lax.all_to_all(hot_down, HOT_COLD, split_axis=1, concat_axis=0, tiled=True)  9.98 us
    all_to_all x1, waiting for transfers between devices, on_device(): lax.all_to_all(up_w, HOT, split_axis=1, concat_axis=0, tiled=True)  9.79 us
  transfers between devices with their start and end apart: 5, of which 2 were waited for; matrix products, arithmetic and copies ran while one was open for 6% of the time, Pallas kernels for 0%

commit v1 on v0

v1 whole, which is shorter than its diff:
```python
import functools

import jax
import jax.numpy as jnp
from jax import lax
from jax.experimental import pallas as pl
from jax.experimental.pallas import tpu as pltpu
from jax.sharding import PartitionSpec as P

MESH = pl.DeviceIdType.MESH
F32 = jnp.float32
BF16 = jnp.bfloat16
RING = 8
HALF = 7
CAP = 14
LANES = 128
EPS = 1e-05
CHUNK = 1024


def silu(v):
    return v / (1.0 + jnp.exp(-v))


def place(index):
    return pl.ds(pl.multiple_of(index * LANES, LANES), LANES)


def kernel(
    tok_hbm,
    gain_hbm,
    hg_hbm,
    hu_hbm,
    hd_hbm,
    hidx_hbm,
    cg_hbm,
    cu_hbm,
    cd_hbm,
    mask_hbm,
    out_ref,
    tok,
    gain,
    hw,
    hidx,
    cg,
    cu,
    cd,
    msk,
    mpad,
    s1,
    r1,
    s2,
    r2,
    h3,
    h4,
    hdp,
    hh,
    zs,
    zr,
    fs,
    fr,
    load_sem,
    own_sem,
    s1_send,
    s1_recv,
    s2_send,
    s2_recv,
    h3_send,
    h3_recv,
    h4_send,
    h4_recv,
    hd_send,
    hd_recv,
    hh_send,
    hh_recv,
    zs_send,
    zs_recv,
    fs_send,
    fs_recv,
):
    hot = lax.axis_index("hot")
    cold = lax.axis_index("cold")
    z = lax.div(hot, RING)
    p = lax.rem(hot, RING)
    seqs, features = tok.shape
    blocks_here = msk.shape[0]

    def ring(base, k):
        return lax.rem(base + k, RING)

    def remote(src, dst, send, recv, hot_to, cold_to):
        return pltpu.make_async_remote_copy(
            src_ref=src,
            dst_ref=dst,
            send_sem=send,
            recv_sem=recv,
            device_id=(hot_to, cold_to),
            device_id_type=MESH,
        )

    loads = [
        (mask_hbm, msk),
        (tok_hbm, tok),
        (gain_hbm, gain),
        (cg_hbm, cg),
        (cu_hbm, cu),
        (hg_hbm, hw.at[pl.ds(0, 16)]),
        (hu_hbm, hw.at[pl.ds(16, 16)]),
        (hidx_hbm, hidx),
        (cd_hbm, cd),
    ]
    load = [
        pltpu.make_async_copy(src, dst, load_sem.at[i])
        for i, (src, dst) in enumerate(loads)
    ]
    for copy in load:
        copy.start()

    def own_piece(zz):
        return pltpu.make_async_copy(
            hd_hbm.at[:, place(zz * RING + p)], hdp.at[p, zz], own_sem.at[zz]
        )

    for zz in range(RING):
        own_piece(zz).start()

    barrier = pltpu.get_barrier_semaphore()
    for k in range(1, RING):
        pl.semaphore_signal(
            barrier, inc=1, device_id=(z * RING + ring(p, k), cold), device_id_type=MESH
        )
        pl.semaphore_signal(
            barrier, inc=1, device_id=(ring(z, k) * RING + p, cold), device_id_type=MESH
        )
    for k in range(1, 4):
        pl.semaphore_signal(
            barrier, inc=1, device_id=(hot, lax.rem(cold + k, 4)), device_id_type=MESH
        )

    load[0].wait()
    mpad[...] = jnp.zeros_like(mpad)
    mpad[0:blocks_here, 0:seqs] = msk[...]
    block_id = lax.broadcasted_iota(jnp.int32, mpad.shape, 0)
    lane_id = lax.broadcasted_iota(jnp.int32, mpad.shape, 1)
    active = mpad[...]
    step = 1
    while step < LANES:
        active = jnp.maximum(active, pltpu.roll(active, step, 1))
        step *= 2
    upto = active
    step = 1
    while step < 32:
        upto = upto + jnp.where(block_id >= step, pltpu.roll(upto, step, 0), 0)
        step *= 2
    ahead = upto - active
    rank = jnp.where(active > 0, ahead, upto[31:32] + block_id - ahead)
    order = jnp.sum(jnp.where(rank == lane_id, block_id, 0), axis=0, keepdims=True)
    slots = [order[0, k] for k in range(CAP)]

    load[1].wait()
    load[2].wait()

    def add_squares(c, total):
        x = tok[:, place(c)].astype(F32)
        return total + x * x

    squares = lax.fori_loop(
        0, features // LANES, add_squares, jnp.zeros((seqs, LANES), F32), unroll=8
    )
    scale = lax.rsqrt(jnp.sum(squares, axis=1, keepdims=True) / features + EPS)
    mine = (tok[:, place(hot)].astype(F32) * scale * gain[:, place(hot)]).astype(BF16)

    load[3].wait()
    load[4].wait()
    for k in range(CAP):
        half, j = divmod(k, HALF)
        cols = pl.ds(slots[k] * LANES, LANES)
        both = jnp.concatenate([cg[:, cols], cu[:, cols]], axis=1)
        part = jnp.dot(mine, both, preferred_element_type=F32).astype(BF16)
        for r in range(4):
            s1[4 * half + r, j, 0] = part[16 * r : 16 * r + 16, :LANES]
            s1[4 * half + r, j, 1] = part[16 * r : 16 * r + 16, LANES:]

    pl.semaphore_wait(barrier, 17)

    def s1_copy(k):
        to = ring(p, k)
        return remote(
            s1.at[to], r1.at[p], s1_send.at[k], s1_recv.at[p], z * RING + to, cold
        )

    for k in range(1, RING):
        s1_copy(k).start()

    def hd_copy(k, zz):
        to = ring(p, k)
        return remote(
            hd_hbm.at[:, place(zz * RING + to)],
            hdp.at[p, zz],
            hd_send.at[k],
            hd_recv.at[p],
            z * RING + to,
            cold,
        )

    for k in range(1, RING):

        @pl.loop(0, RING)
        def _(zz):
            hd_copy(k, zz).start()

    load[5].wait()
    load[6].wait()

    def hot_chunk(c, total):
        cols = pl.ds(pl.multiple_of(c * CHUNK, CHUNK), CHUNK)
        normed = (tok[:, cols].astype(F32) * scale * gain[:, cols]).astype(BF16)
        return total + lax.dot_general(
            hw[:, cols], normed, (((1,), (1,)), ((), ())), preferred_element_type=F32
        )

    hot_t = lax.fori_loop(
        0, features // CHUNK, hot_chunk, jnp.zeros((32, seqs), F32)
    )
    hidden_t = silu(hot_t[:16]) * hot_t[16:]
    hh[p] = jnp.concatenate([hidden_t, jnp.zeros_like(hidden_t)], axis=1).astype(BF16)

    def hh_copy(k):
        to = ring(p, k)
        return remote(
            hh.at[p], hh.at[p], hh_send.at[k], hh_recv.at[p], z * RING + to, cold
        )

    for k in range(1, RING):
        hh_copy(k).start()

    busy = z != p
    j_own = lax.rem(z - p - 1 + 2 * RING, RING)
    half_own = lax.div(p, 4)
    row_own = lax.rem(p, 4)
    slot_own = half_own * HALF + j_own
    block_own = jnp.int32(0)
    for k in range(CAP):
        block_own = jnp.where(slot_own == k, slots[k], block_own)
    load[7].wait()
    unit = (cold * blocks_here + block_own) * LANES + lax.broadcasted_iota(
        jnp.int32, (LANES, LANES), 0
    )

    def match(c, found):
        return jnp.where(hidx[:, place(c)] == unit, 1.0, found)

    found = lax.fori_loop(
        0, hidx.shape[1] // LANES, match, jnp.zeros((LANES, LANES), F32), unroll=4
    )
    hot_units = lax.dot_general(
        jnp.ones((8, LANES), BF16),
        found.astype(BF16),
        (((1,), (1,)), ((), ())),
        preferred_element_type=F32,
    )[0:1]
    chosen = jnp.sum(
        jnp.where(block_id == block_own, mpad[...], 0).astype(F32), axis=0, keepdims=True
    )
    row = lax.broadcasted_iota(jnp.int32, (16, LANES), 0) + row_own * 16
    column = lax.broadcasted_iota(jnp.int32, (16, LANES), 1)
    seq_live = jnp.sum(jnp.where(row == column, chosen, 0.0), axis=1, keepdims=True)
    live = seq_live * (1.0 - jnp.minimum(hot_units, 1.0))

    total = s1[p].astype(F32)
    for k in range(1, RING):
        src = ring(p, k)
        remote(
            s1.at[src], r1.at[src], s1_send.at[k], s1_recv.at[src], z * RING + src, cold
        ).wait_recv()
        total = total + r1[src].astype(F32)
    s2[...] = total.astype(BF16)

    def s2_copy(j):
        to = ring(p, 1 + j)
        return to, remote(
            s2.at[j], r2.at[z], s2_send.at[j], s2_recv.at[z], to * RING + p, cold
        )

    for j in range(HALF):
        to, copy = s2_copy(j)

        @pl.when(to != z)
        def _():
            copy.start()

    for zz in range(RING):
        own_piece(zz).wait()
    for k in range(1, RING):
        src = ring(p, k)
        remote(
            hdp.at[src], hdp.at[src], hd_send.at[k], hd_recv.at[src], z * RING + src, cold
        ).wait_recv()
        remote(
            hh.at[src], hh.at[src], hh_send.at[k], hh_recv.at[src], z * RING + src, cold
        ).wait_recv()
    hidden = jnp.transpose(hh[...].reshape(LANES, LANES).astype(F32))[:seqs].astype(BF16)
    for zz in range(0, RING, 2):
        down = jnp.concatenate(
            [
                hdp[:, zz].reshape(LANES, LANES),
                hdp[:, zz + 1].reshape(LANES, LANES),
            ],
            axis=1,
        )
        part = jnp.dot(hidden, down, preferred_element_type=F32).astype(BF16)
        zs[zz] = part[:, :LANES]
        zs[zz + 1] = part[:, LANES:]

    def zs_copy(k):
        to = ring(z, k)
        return remote(
            zs.at[to], zr.at[z], zs_send.at[k], zs_recv.at[z], to * RING + p, cold
        )

    for k in range(1, RING):
        zs_copy(k).start()

    def h3_copy(k):
        to = ring(z, k)
        return remote(
            h3.at[j_own],
            h3.at[j_own],
            h3_send.at[k],
            h3_recv.at[j_own],
            to * RING + p,
            cold,
        )

    @pl.when(busy)
    def _():
        both = s2[j_own].astype(F32)
        for k in range(1, RING):
            src = ring(z, k)
            remote(
                r2.at[src], r2.at[src], s2_send.at[0], s2_recv.at[src], src * RING + p, cold
            ).wait_recv()
            both = both + r2[src].astype(F32)
        h3[j_own] = (silu(both[0]) * both[1] * live).astype(BF16)
        for k in range(1, RING):
            h3_copy(k).start()

    hot_out = zs[z].astype(F32)
    for k in range(1, RING):
        src = ring(z, k)
        remote(
            zr.at[src], zr.at[src], zs_send.at[k], zs_recv.at[src], src * RING + p, cold
        ).wait_recv()
        hot_out = hot_out + zr[src].astype(F32)

    for j in range(HALF):
        src = ring(p, 1 + j)

        @pl.when(src != z)
        def _():
            remote(
                h3.at[j], h3.at[j], h3_send.at[1 + j], h3_recv.at[j], src * RING + p, cold
            ).wait_recv()

    def h4_copy(k):
        to = ring(p, k)
        return remote(
            h3, h4.at[p], h4_send.at[k], h4_recv.at[p], z * RING + to, cold
        )

    for k in range(1, RING):
        h4_copy(k).start()
    h4[p] = h3[...]
    load[8].wait()
    for k in range(1, RING):
        src = ring(p, k)
        remote(
            h3, h4.at[src], h4_send.at[k], h4_recv.at[src], z * RING + src, cold
        ).wait_recv()

    acc = hot_out
    for k in range(0, CAP, 2):
        left, right = [
            h4[4 * (i // HALF) : 4 * (i // HALF) + 4, i % HALF].reshape(seqs, LANES)
            for i in (k, k + 1)
        ]
        down = jnp.concatenate(
            [cd[pl.ds(slots[i] * LANES, LANES), :] for i in (k, k + 1)], axis=0
        )
        acc = acc + jnp.dot(
            jnp.concatenate([left, right], axis=1), down, preferred_element_type=F32
        )

    flipped = jnp.transpose(jnp.concatenate([acc, jnp.zeros_like(acc)], axis=0))
    for c in range(4):
        fs[c] = jnp.concatenate(
            [
                flipped[32 * c : 32 * c + 16, :seqs],
                flipped[32 * c + 16 : 32 * c + 32, :seqs],
            ],
            axis=1,
        )

    def fs_copy(k):
        to = lax.rem(cold + k, 4)
        return remote(fs.at[to], fr.at[cold], fs_send.at[k], fs_recv.at[cold], hot, to)

    for k in range(1, 4):
        fs_copy(k).start()
    result = fs[cold]
    for k in range(1, 4):
        src = lax.rem(cold + k, 4)
        remote(
            fr.at[src], fr.at[src], fs_send.at[k], fs_recv.at[src], hot, src
        ).wait_recv()
        result = result + fr[src]
    out_ref[0:16, :] = result[:, :seqs].astype(BF16)
    out_ref[16:32, :] = result[:, seqs:].astype(BF16)

    for k in range(1, RING):
        s1_copy(k).wait_send()
        remote(
            hdp.at[p], hdp.at[p], hd_send.at[k], hd_recv.at[p], z * RING + ring(p, k), cold
        ).wait_send()
        hh_copy(k).wait_send()
        zs_copy(k).wait_send()
        h4_copy(k).wait_send()
    for j in range(HALF):
        to, copy = s2_copy(j)

        @pl.when(to != z)
        def _():
            copy.wait_send()

    @pl.when(busy)
    def _():
        for k in range(1, RING):
            h3_copy(k).wait_send()

    for k in range(1, 4):
        fs_copy(k).wait_send()


def on_device(
    tokens,
    norm_gain,
    hot_gate,
    hot_up,
    hot_down,
    hot_index,
    cold_gate,
    cold_up,
    cold_down,
    block_mask,
):
    seqs, features = tokens.shape
    dma = pltpu.SemaphoreType.DMA
    any_space = pl.BlockSpec(memory_space=pl.ANY)
    return pl.pallas_call(
        kernel,
        out_shape=jax.ShapeDtypeStruct((32, seqs), BF16),
        in_specs=[any_space] * 10,
        out_specs=pl.BlockSpec(memory_space=pltpu.VMEM),
        scratch_shapes=[
            pltpu.VMEM(tokens.shape, BF16),
            pltpu.VMEM((1, features), F32),
            pltpu.VMEM((32, features), BF16),
            pltpu.VMEM((1, hot_index.shape[0]), jnp.int32),
            pltpu.VMEM(cold_gate.shape, BF16),
            pltpu.VMEM(cold_up.shape, BF16),
            pltpu.VMEM(cold_down.shape, BF16),
            pltpu.VMEM(block_mask.shape[::-1], jnp.int32),
            pltpu.VMEM((32, LANES), jnp.int32),
            pltpu.VMEM((RING, HALF, 2, 16, LANES), BF16),
            pltpu.VMEM((RING, HALF, 2, 16, LANES), BF16),
            pltpu.VMEM((HALF, 2, 16, LANES), BF16),
            pltpu.VMEM((RING, 2, 16, LANES), BF16),
            pltpu.VMEM((HALF, 16, LANES), BF16),
            pltpu.VMEM((RING, HALF, 16, LANES), BF16),
            pltpu.VMEM((RING, RING, 16, LANES), BF16),
            pltpu.VMEM((RING, 16, LANES), BF16),
            pltpu.VMEM((RING, seqs, LANES), BF16),
            pltpu.VMEM((RING, seqs, LANES), BF16),
            pltpu.VMEM((4, 16, LANES), F32),
            pltpu.VMEM((4, 16, LANES), F32),
            dma((9,)),
            dma((RING,)),
        ]
        + [dma((RING,))] * 14
        + [dma((4,))] * 2,
        compiler_params=pltpu.CompilerParams(collective_id=0, has_side_effects=True),
    )(
        tokens,
        norm_gain.reshape(1, -1),
        hot_gate,
        hot_up,
        hot_down,
        hot_index.reshape(1, -1),
        cold_gate,
        cold_up,
        cold_down,
        block_mask.T,
    ).T


def solution(mesh):
    rows = P(("hot", "cold"), None)
    return jax.shard_map(
        on_device,
        mesh=mesh,
        in_specs=(
            P(),
            P(),
            rows,
            rows,
            rows,
            P(),
            P("hot", "cold"),
            P("hot", "cold"),
            P("cold", "hot"),
            P(None, "cold"),
        ),
        out_specs=P(None, ("hot", "cold")),
        check_vma=False,
    )
```

time: 461 us -> 41 us (0.09)
  blocking collectives: 297 us -> 0 us
  starting transfers between devices: 100 us -> 0 us
  Pallas kernels: 0 us -> 39.4 us
  local copies, waits for them, and re-layouts: 37.9 us -> 1.3 us
  waiting for transfers between devices: 18.7 us -> 0 us
    all_gather x2 -> x0, blocking collectives: 297 us -> none  [all_blocks(): pieces = lax.all_gather(pieces, axes[k])]
    all_to_all x5 -> x0, starting transfers between devices: 100 us -> none  [the longest x1 58.8 us: summed_on_arrival(): lax.all_to_all(pieces, axis, split_axis=0, concat_axis=0, tiled=True)]
    pallas_call x0 -> x1, Pallas kernels: none -> 39.4 us  [on_device(): pl.pallas_call(kernel, out_shape=jax.ShapeDtypeStruct((32, seqs), BF16),...]
    all_to_all x5 -> x0, waiting for transfers between devices: 18.7 us -> none  [the longest x1 9.79 us: on_device(): lax.all_to_all(up_w, HOT, split_axis=1, concat_axis=0, tiled=True)]
    scatter x1 -> x0, local copies, waits for them, and re-layouts: 15.5 us -> none  [on_device(): is_hot = jnp.zeros((UNITS,), jnp.float32).at[hot_index].set(1.0)]
    unnamed x33 -> x1, local copies, waits for them, and re-layouts: 7.92 us -> 1.3 us
    all_to_all x8 -> x0, local copies, waits for them, and re-layouts: 6 us -> none  [the longest x3 2.32 us: on_device(): lax.all_to_all(hot_down, HOT_COLD, split_axis=1, concat_axis=0, tiled=True)]
  transfers between devices with their start and end apart: 5 -> 0, of which waited for: 2 -> 0; matrix products, arithmetic and copies ran while one was open for 6% -> 0% of each run, Pallas kernels for 0% -> 0%
where the time goes in v1:
time: 41 us; the launch traced here: 40.8 us
  Pallas kernels  39.4 us (96%)
  local copies, waits for them, and re-layouts  1.3 us (3%)
    pallas_call x1, Pallas kernels, on_device(): pl.pallas_call(kernel, out_shape=jax.ShapeDtypeStruct((32, seqs), BF16),...  39.4 us
    unnamed x1, local copies, waits for them, and re-layouts  1.3 us

profile of v1, /device:TPU:1, one launch (start us, length us, event | category | flops | bytes accessed | tf_op | source)
XLA Modules:
  0.0 40.8 jit_solution(17982724152422298092)
XLA Ops:
  0.0 39.4 %shard_map.100 = bf16[32,64]{1,0:T(8,128)(2,1)} custom-call(bf16[64,8192]{1,0:T(8,128)(2,1)} %tok_hbm.1, f32[1,8192]{1,0:T(1,128)} %bitcast.4, bf16[16,8192]{1,0:T(8,128)(2,1)} %hg_hbm.1, bf16[16,8192]{1,0:T(8,128)(2,1)} %hu_hbm.1, bf16[16,8192]{1,0:T(8,128)(2,1)} %hd_hbm.1, s32[1,4096]{1,0:T(1,128)} %bitcast.6, bf16[128,3584]{1,0:T(8,128)(2,1)} %cg_hbm.1, ...), custom_call_target="tpu_custom_call" | custom-call | tf_op jit(solution)/shard_map/pallas_call | solution.py:459
  39.5 1.3 %copy.12 = bf16[64,32]{0,1:T(8,128)(2,1)} copy(bf16[64,32]{0,1:T(8,128)(2,1)} %bitcast.5) | data formatting | bytes 8192

commit v2 on v1

v2 whole, which is shorter than its diff:
```python
import functools

import jax
import jax.numpy as jnp
from jax import lax
from jax.experimental import pallas as pl
from jax.experimental.pallas import tpu as pltpu
from jax.sharding import PartitionSpec as P

MESH = pl.DeviceIdType.MESH
F32 = jnp.float32
BF16 = jnp.bfloat16
RING = 8
PAIRS = 7
CAP = 14
LANES = 128
EPS = 1e-05
CHUNK = 1024


def silu(v):
    return v / (1.0 + jnp.exp(-v))


def place(index):
    return pl.ds(pl.multiple_of(index * LANES, LANES), LANES)


def kernel(
    tok_hbm,
    gain_hbm,
    hg_hbm,
    hu_hbm,
    hd_hbm,
    hidx_hbm,
    cg_hbm,
    cu_hbm,
    cd_hbm,
    mask_hbm,
    out_ref,
    tok,
    gain,
    hw,
    hidx,
    cg,
    cu,
    cd,
    msk,
    mpad,
    s1,
    r1,
    s2,
    r2,
    h3,
    cds,
    cdr,
    hdp,
    hh,
    acc,
    fs,
    fr,
    load_sem,
    own_sem,
    s1_send,
    s1_recv,
    s2_send,
    s2_recv,
    h3_send,
    h3_recv,
    cd_send,
    cd_recv,
    hd_send,
    hd_recv,
    hh_send,
    hh_recv,
    fs_send,
    fs_recv,
):
    hot = lax.axis_index("hot")
    cold = lax.axis_index("cold")
    z = lax.div(hot, RING)
    p = lax.rem(hot, RING)
    core = lax.rem(cold, 2)
    seqs, features = tok.shape
    blocks_here = msk.shape[0]

    def ring(base, k):
        return lax.rem(base + k, RING)

    def swap(place_or_pair):
        return place_or_pair + core * (1 - 2 * lax.rem(place_or_pair, 2))

    pair = swap(p)
    works = pair < PAIRS

    def remote(src, dst, send, recv, hot_to, cold_to):
        return pltpu.make_async_remote_copy(
            src_ref=src,
            dst_ref=dst,
            send_sem=send,
            recv_sem=recv,
            device_id=(hot_to, cold_to),
            device_id_type=MESH,
        )

    def in_plane(to):
        return z * RING + to

    def along_z(to):
        return to * RING + p

    loads = [
        (mask_hbm, msk),
        (tok_hbm, tok),
        (gain_hbm, gain),
        (cg_hbm, cg),
        (cu_hbm, cu),
        (hg_hbm, hw.at[pl.ds(0, 16)]),
        (hu_hbm, hw.at[pl.ds(16, 16)]),
        (hidx_hbm, hidx),
        (cd_hbm, cd),
    ]
    load = [
        pltpu.make_async_copy(src, dst, load_sem.at[i])
        for i, (src, dst) in enumerate(loads)
    ]
    for copy in load:
        copy.start()

    def columns_of(zz):
        return pl.ds(pl.multiple_of(zz * RING * LANES, RING * LANES), RING * LANES)

    own_piece = pltpu.make_async_copy(
        hd_hbm.at[:, columns_of(z)], hdp.at[z], own_sem.at[0]
    )
    own_piece.start()

    barrier = pltpu.get_barrier_semaphore()

    def greet(hot_to, cold_to):
        pl.semaphore_signal(
            barrier, inc=1, device_id=(hot_to, cold_to), device_id_type=MESH
        )

    for k in range(1, RING):
        greet(along_z(ring(z, k)), cold)
    for k in range(RING):
        for c in range(4):
            if k + c:
                greet(in_plane(ring(p, k)), lax.rem(cold + c, 4))

    load[0].wait()
    mpad[...] = jnp.zeros_like(mpad)
    mpad[0:blocks_here, 0:seqs] = msk[...]
    block_id = lax.broadcasted_iota(jnp.int32, mpad.shape, 0)
    lane_id = lax.broadcasted_iota(jnp.int32, mpad.shape, 1)
    active = mpad[...]
    step = 1
    while step < LANES:
        active = jnp.maximum(active, pltpu.roll(active, step, 1))
        step *= 2
    upto = active
    step = 1
    while step < 32:
        upto = upto + jnp.where(block_id >= step, pltpu.roll(upto, step, 0), 0)
        step *= 2
    ahead = upto - active
    rank = jnp.where(active > 0, ahead, upto[31:32] + block_id - ahead)
    order = jnp.sum(jnp.where(rank == lane_id, block_id, 0), axis=0, keepdims=True)
    slots = [order[0, k] for k in range(CAP)]

    load[1].wait()
    load[2].wait()

    def add_squares(c, total):
        x = tok[:, place(c)].astype(F32)
        return total + x * x

    squares = lax.fori_loop(
        0, features // LANES, add_squares, jnp.zeros((seqs, LANES), F32), unroll=8
    )
    scale = lax.rsqrt(jnp.sum(squares, axis=1, keepdims=True) / features + EPS)
    mine = (tok[:, place(hot)].astype(F32) * scale * gain[:, place(hot)]).astype(BF16)

    load[3].wait()
    load[4].wait()
    for k in range(CAP):
        cols = pl.ds(slots[k] * LANES, LANES)
        both = jnp.concatenate([cg[:, cols], cu[:, cols]], axis=1)
        part = jnp.dot(mine, both, preferred_element_type=F32).astype(BF16)
        s1[k // 2, k % 2, 0] = part[:, :LANES]
        s1[k // 2, k % 2, 1] = part[:, LANES:]

    pl.semaphore_wait(barrier, 38)

    def s1_copy(k):
        to = ring(p, k)
        at = jnp.minimum(swap(to), PAIRS - 1)
        return to, remote(
            s1.at[at], r1.at[p], s1_send.at[k], s1_recv.at[p], in_plane(to), cold
        )

    def hd_copy(k):
        to = ring(z, k)
        return remote(
            hd_hbm.at[:, columns_of(to)],
            hdp.at[z],
            hd_send.at[k],
            hd_recv.at[z],
            along_z(to),
            cold,
        )

    for k in range(1, RING):
        to, copy = s1_copy(k)

        @pl.when(swap(to) < PAIRS)
        def _():
            copy.start()

    for k in range(1, RING):
        hd_copy(k).start()

    load[5].wait()
    load[6].wait()

    def hot_chunk(c, total):
        cols = pl.ds(pl.multiple_of(c * CHUNK, CHUNK), CHUNK)
        normed = (tok[:, cols].astype(F32) * scale * gain[:, cols]).astype(BF16)
        return total + lax.dot_general(
            hw[:, cols], normed, (((1,), (1,)), ((), ())), preferred_element_type=F32
        )

    hot_t = lax.fori_loop(
        0, features // CHUNK, hot_chunk, jnp.zeros((32, seqs), F32)
    )
    hidden_t = silu(hot_t[:16]) * hot_t[16:]
    hh[z] = jnp.concatenate([hidden_t, jnp.zeros_like(hidden_t)], axis=1).astype(BF16)

    def hh_copy(k):
        return remote(
            hh.at[z], hh.at[z], hh_send.at[k], hh_recv.at[z], along_z(ring(z, k)), cold
        )

    for k in range(1, RING):
        hh_copy(k).start()

    half = lax.rem(z, 2)
    rows = lax.div(z, 2)
    slot_own = jnp.minimum(pair, PAIRS - 1) * 2 + half
    block_own = jnp.int32(0)
    for k in range(CAP):
        block_own = jnp.where(slot_own == k, slots[k], block_own)
    load[7].wait()
    unit = (cold * blocks_here + block_own) * LANES + lax.broadcasted_iota(
        jnp.int32, (LANES, LANES), 0
    )

    def match(c, found):
        return jnp.where(hidx[:, place(c)] == unit, 1.0, found)

    found = lax.fori_loop(
        0, hidx.shape[1] // LANES, match, jnp.zeros((LANES, LANES), F32), unroll=4
    )
    hot_units = lax.dot_general(
        jnp.ones((8, LANES), BF16),
        found.astype(BF16),
        (((1,), (1,)), ((), ())),
        preferred_element_type=F32,
    )[0:1]
    chosen = jnp.sum(
        jnp.where(block_id == block_own, mpad[...], 0).astype(F32), axis=0, keepdims=True
    )
    row = lax.broadcasted_iota(jnp.int32, (16, LANES), 0) + rows * 16
    column = lax.broadcasted_iota(jnp.int32, (16, LANES), 1)
    seq_live = jnp.sum(jnp.where(row == column, chosen, 0.0), axis=1, keepdims=True)
    live = seq_live * (1.0 - jnp.minimum(hot_units, 1.0))

    load[8].wait()
    for k in range(CAP):
        block = cd[pl.ds(slots[k] * LANES, LANES), :]
        cds[k // 2, :, LANES * (k % 2) : LANES * (k % 2) + LANES] = jnp.transpose(block)

    @pl.when(works)
    def _():
        total = s1[jnp.minimum(pair, PAIRS - 1)].astype(F32)
        for k in range(1, RING):
            src = ring(p, k)
            remote(
                s1.at[0], r1.at[src], s1_send.at[k], s1_recv.at[src], in_plane(src), cold
            ).wait_recv()
            total = total + r1[src].astype(F32)
        total = total.astype(BF16)
        for r in range(4):
            for e in range(2):
                for g in range(2):
                    s2[2 * r + e, g] = total[e, g, 16 * r : 16 * r + 16]

    def s2_copy(k):
        to = ring(z, k)
        return remote(
            s2.at[to], r2.at[z], s2_send.at[k], s2_recv.at[z], along_z(to), cold
        )

    @pl.when(works)
    def _():
        for k in range(1, RING):
            s2_copy(k).start()

    def cd_copy(k):
        to = ring(p, k)
        at = jnp.minimum(swap(to), PAIRS - 1)
        return to, remote(
            cds.at[at], cdr.at[p], cd_send.at[k], cd_recv.at[p], in_plane(to), cold
        )

    for k in range(1, RING):
        to, copy = cd_copy(k)

        @pl.when(swap(to) < PAIRS)
        def _():
            copy.start()

    cdr[p] = cds[jnp.minimum(pair, PAIRS - 1)]

    piece = half * 4 + rows

    def h3_copy(k):
        return remote(
            h3.at[piece],
            h3.at[piece],
            h3_send.at[k],
            h3_recv.at[z],
            along_z(ring(z, k)),
            cold,
        )

    @pl.when(works)
    def _():
        both = s2[z].astype(F32)
        for k in range(1, RING):
            src = ring(z, k)
            remote(
                s2.at[src], r2.at[src], s2_send.at[k], s2_recv.at[src], along_z(src), cold
            ).wait_recv()
            both = both + r2[src].astype(F32)
        h3[piece] = (silu(both[0]) * both[1] * live).astype(BF16)
        for k in range(1, RING):
            h3_copy(k).start()

    own_piece.wait()
    for k in range(1, RING):
        src = ring(z, k)
        remote(
            hdp.at[src], hdp.at[src], hd_send.at[k], hd_recv.at[src], along_z(src), cold
        ).wait_recv()
        remote(
            hh.at[src], hh.at[src], hh_send.at[k], hh_recv.at[src], along_z(src), cold
        ).wait_recv()
    hidden = hh[...].reshape(LANES, LANES)[:, :seqs]
    for q in range(RING):
        down = hdp[:, :, LANES * q : LANES * q + LANES].reshape(LANES, LANES)
        acc[q] = jnp.dot(jnp.transpose(down), hidden, preferred_element_type=F32)

    @pl.when(works)
    def _():
        for k in range(1, RING):
            src = ring(p, k)
            remote(
                cds.at[0], cdr.at[src], cd_send.at[k], cd_recv.at[src], in_plane(src), cold
            ).wait_recv()

    @pl.when(works)
    def _():
        for k in range(1, RING):
            src = ring(z, k)
            remote(
                h3.at[piece], h3.at[piece], h3_send.at[k], h3_recv.at[src], along_z(src), cold
            ).wait_recv()

    @pl.when(works)
    def _():
        pair_hidden = jnp.concatenate(
            [h3[0:4].reshape(seqs, LANES), h3[4:8].reshape(seqs, LANES)], axis=1
        )
        for q in range(RING):
            acc[q] = acc[q] + lax.dot_general(
                cdr[q],
                pair_hidden,
                (((1,), (1,)), ((), ())),
                preferred_element_type=F32,
            )

    for q in range(RING):
        for c in range(4):
            fs[q, c] = jnp.concatenate(
                [acc[q, 32 * c : 32 * c + 16, :], acc[q, 32 * c + 16 : 32 * c + 32, :]],
                axis=1,
            ).astype(BF16)

    def fs_copy(k, c):
        to, cold_to = ring(p, k), lax.rem(cold + c, 4)
        return remote(
            fs.at[to, cold_to],
            fr.at[k * 4 + c - 1],
            fs_send,
            fs_recv,
            in_plane(to),
            cold_to,
        )

    others = [(k, c) for k in range(RING) for c in range(4) if k + c]
    for k, c in others:
        fs_copy(k, c).start()

    result = fs[p, cold].astype(F32)
    all_others = pltpu.make_async_copy(fr, fr, fs_recv)
    all_others.wait()
    for i in range(len(others)):
        result = result + fr[i].astype(F32)
    out_ref[0:16, :] = result[:, :seqs].astype(BF16)
    out_ref[16:32, :] = result[:, seqs:].astype(BF16)

    pltpu.make_async_copy(fr, fr, fs_send).wait()
    for k in range(1, RING):
        hd_copy(k).wait_send()
        hh_copy(k).wait_send()
        for to, copy in (s1_copy(k), cd_copy(k)):

            @pl.when(swap(to) < PAIRS)
            def _():
                copy.wait_send()

    @pl.when(works)
    def _():
        for k in range(1, RING):
            s2_copy(k).wait_send()
            h3_copy(k).wait_send()


def on_device(
    tokens,
    norm_gain,
    hot_gate,
    hot_up,
    hot_down,
    hot_index,
    cold_gate,
    cold_up,
    cold_down,
    block_mask,
):
    seqs, features = tokens.shape
    dma = pltpu.SemaphoreType.DMA
    any_space = pl.BlockSpec(memory_space=pl.ANY)
    return pl.pallas_call(
        kernel,
        out_shape=jax.ShapeDtypeStruct((32, seqs), BF16),
        in_specs=[any_space] * 10,
        out_specs=pl.BlockSpec(memory_space=pltpu.VMEM),
        scratch_shapes=[
            pltpu.VMEM(tokens.shape, BF16),
            pltpu.VMEM((1, features), F32),
            pltpu.VMEM((32, features), BF16),
            pltpu.VMEM((1, hot_index.shape[0]), jnp.int32),
            pltpu.VMEM(cold_gate.shape, BF16),
            pltpu.VMEM(cold_up.shape, BF16),
            pltpu.VMEM(cold_down.shape, BF16),
            pltpu.VMEM(block_mask.shape[::-1], jnp.int32),
            pltpu.VMEM((32, LANES), jnp.int32),
            pltpu.VMEM((PAIRS, 2, 2, seqs, LANES), BF16),
            pltpu.VMEM((RING, 2, 2, seqs, LANES), BF16),
            pltpu.VMEM((RING, 2, 16, LANES), BF16),
            pltpu.VMEM((RING, 2, 16, LANES), BF16),
            pltpu.VMEM((RING, 16, LANES), BF16),
            pltpu.VMEM((PAIRS, LANES, 2 * LANES), BF16),
            pltpu.VMEM((RING, LANES, 2 * LANES), BF16),
            pltpu.VMEM((RING, 16, RING * LANES), BF16),
            pltpu.VMEM((RING, 16, LANES), BF16),
            pltpu.VMEM((RING, LANES, seqs), F32),
            pltpu.VMEM((RING, 4, 16, LANES), BF16),
            pltpu.VMEM((RING * 4 - 1, 16, LANES), BF16),
            dma((9,)),
            dma((1,)),
        ]
        + [dma((RING,))] * 12
        + [dma, dma],
        compiler_params=pltpu.CompilerParams(collective_id=0, has_side_effects=True),
    )(
        tokens,
        norm_gain.reshape(1, -1),
        hot_gate,
        hot_up,
        hot_down,
        hot_index.reshape(1, -1),
        cold_gate,
        cold_up,
        cold_down,
        block_mask.T,
    ).T


def solution(mesh):
    rows = P(("hot", "cold"), None)
    return jax.shard_map(
        on_device,
        mesh=mesh,
        in_specs=(
            P(),
            P(),
            rows,
            rows,
            rows,
            P(),
            P("hot", "cold"),
            P("hot", "cold"),
            P("cold", "hot"),
            P(None, "cold"),
        ),
        out_specs=P(None, ("hot", "cold")),
        check_vma=False,
    )
```

time: 41 us -> 38.7 us (0.944)
  Pallas kernels: 39.4 us -> 37.2 us
    pallas_call x1, Pallas kernels: 39.4 us -> 37.2 us  [on_device(): pl.pallas_call(kernel, out_shape=jax.ShapeDtypeStruct((32, seqs), BF16),...]
where the time goes in v2:
time: 38.7 us; the launch traced here: 38.5 us
  Pallas kernels  37.2 us (96%)
  local copies, waits for them, and re-layouts  1.3 us (3%)
    pallas_call x1, Pallas kernels, on_device(): pl.pallas_call(kernel, out_shape=jax.ShapeDtypeStruct((32, seqs), BF16),...  37.2 us
    unnamed x1, local copies, waits for them, and re-layouts  1.3 us

profile of v2, /device:TPU:1, one launch (start us, length us, event | category | flops | bytes accessed | tf_op | source)
XLA Modules:
  0.0 38.5 jit_solution(11030538277686414358)
XLA Ops:
  0.0 37.2 %shard_map.100 = bf16[32,64]{1,0:T(8,128)(2,1)} custom-call(bf16[64,8192]{1,0:T(8,128)(2,1)} %tok_hbm.1, f32[1,8192]{1,0:T(1,128)} %bitcast.4, bf16[16,8192]{1,0:T(8,128)(2,1)} %hg_hbm.1, bf16[16,8192]{1,0:T(8,128)(2,1)} %hu_hbm.1, bf16[16,8192]{1,0:T(8,128)(2,1)} %hd_hbm.1, s32[1,4096]{1,0:T(1,128)} %bitcast.6, bf16[128,3584]{1,0:T(8,128)(2,1)} %cg_hbm.1, ...), custom_call_target="tpu_custom_call" | custom-call | tf_op jit(solution)/shard_map/pallas_call | solution.py:456
  37.2 1.3 %copy.12 = bf16[64,32]{0,1:T(8,128)(2,1)} copy(bf16[64,32]{0,1:T(8,128)(2,1)} %bitcast.5) | data formatting | bytes 8192

commit v3 on v2

v3 whole, which is shorter than its diff:
```python
import functools

import jax
import jax.numpy as jnp
from jax import lax
from jax.experimental import pallas as pl
from jax.experimental.pallas import tpu as pltpu
from jax.sharding import PartitionSpec as P

MESH = pl.DeviceIdType.MESH
F32 = jnp.float32
BF16 = jnp.bfloat16
RING = 8
FAR_Z = (4, 3, 5, 2, 6, 1, 7)
FAR_PLANE = (5, 4, 3, 7, 2, 6, 1)
PAIRS = 7
CAP = 14
LANES = 128
EPS = 1e-05
CHUNK = 1024


def silu(v):
    return v / (1.0 + jnp.exp(-v))


def place(index):
    return pl.ds(pl.multiple_of(index * LANES, LANES), LANES)


def kernel(
    tok_hbm,
    gain_hbm,
    hg_hbm,
    hu_hbm,
    hd_hbm,
    hidx_hbm,
    cg_hbm,
    cu_hbm,
    cd_hbm,
    mask_hbm,
    out_ref,
    tok,
    gain,
    hw,
    hidx,
    cg,
    cu,
    cd,
    msk,
    mpad,
    s1,
    r1,
    s2,
    r2,
    h3,
    cds,
    cdr,
    hdp,
    hh,
    lv,
    acc,
    fs,
    fr,
    load_sem,
    own_sem,
    s1_send,
    s1_recv,
    s2_send,
    s2_recv,
    h3_send,
    h3_recv,
    cd_send,
    cd_recv,
    hd_send,
    hd_recv,
    hh_send,
    hh_recv,
    lv_send,
    lv_recv,
    fs_send,
    fs_recv,
):
    hot = lax.axis_index("hot")
    cold = lax.axis_index("cold")
    z = lax.div(hot, RING)
    p = lax.rem(hot, RING)
    x_hi = lax.div(cold, 2)
    core = lax.rem(cold, 2)
    adds = core == 1
    partner = x_hi * 2 + 1
    seqs, features = tok.shape
    blocks_here = msk.shape[0]

    def ring(base, k):
        return lax.rem(base + k, RING)

    def in_plane_at(k):
        dy, dx = divmod(k, 2)
        y, x = lax.div(p, 2), lax.rem(p, 2)
        return tuple(
            lax.rem(y + d, 4) * 2 + x + dx * (1 - 2 * x) for d in (dy, 4 - dy)
        )

    def swap(group, place_or_pair):
        return place_or_pair + group * (1 - 2 * lax.rem(place_or_pair, 2))

    def works(group):
        return swap(group, p) < PAIRS

    def pair_of(group, to):
        return jnp.minimum(swap(group, to), PAIRS - 1)

    def remote(src, dst, send, recv, hot_to, cold_to):
        return pltpu.make_async_remote_copy(
            src_ref=src,
            dst_ref=dst,
            send_sem=send,
            recv_sem=recv,
            device_id=(hot_to, cold_to),
            device_id_type=MESH,
        )

    def in_plane(to):
        return z * RING + to

    def along_z(to):
        return to * RING + p

    loads = [
        (mask_hbm, msk),
        (tok_hbm, tok),
        (gain_hbm, gain),
        (cg_hbm, cg),
        (cu_hbm, cu),
        (hg_hbm, hw.at[pl.ds(0, 16)]),
        (hu_hbm, hw.at[pl.ds(16, 16)]),
        (hidx_hbm, hidx),
        (cd_hbm, cd),
    ]
    load = [
        pltpu.make_async_copy(src, dst, load_sem.at[i])
        for i, (src, dst) in enumerate(loads)
    ]
    for copy in load:
        copy.start()

    def columns_of(zz):
        return pl.ds(pl.multiple_of(zz * RING * LANES, RING * LANES), RING * LANES)

    own_piece = pltpu.make_async_copy(
        hd_hbm.at[:, columns_of(z)], hdp.at[1, z], own_sem.at[0]
    )

    @pl.when(adds)
    def _():
        own_piece.start()

    barrier = pltpu.get_barrier_semaphore()

    def greet(hot_to, cold_to):
        pl.semaphore_signal(
            barrier, inc=1, device_id=(hot_to, cold_to), device_id_type=MESH
        )

    for k in FAR_Z:
        greet(along_z(ring(z, k)), partner)
    for k in FAR_PLANE:
        greet(in_plane(in_plane_at(k)[0]), partner)
        greet(in_plane(in_plane_at(k)[0]), (1 - x_hi) * 2 + 1)
    greet(hot, (1 - x_hi) * 2 + 1)

    @pl.when(adds)
    def _():
        for k in FAR_Z:
            greet(along_z(ring(z, k)), x_hi * 2)
        for k in (*FAR_PLANE, 0):
            greet(in_plane(in_plane_at(k)[0]), x_hi * 2)
            greet(in_plane(in_plane_at(k)[0]), (1 - x_hi) * 2)

    @pl.when(core == 0)
    def _():
        greet(hot, partner)

    load[0].wait()
    mpad[...] = jnp.zeros_like(mpad)
    mpad[0:blocks_here, 0:seqs] = msk[...]
    block_id = lax.broadcasted_iota(jnp.int32, mpad.shape, 0)
    lane_id = lax.broadcasted_iota(jnp.int32, mpad.shape, 1)
    active = mpad[...]
    step = 1
    while step < LANES:
        active = jnp.maximum(active, pltpu.roll(active, step, 1))
        step *= 2
    upto = active
    step = 1
    while step < 32:
        upto = upto + jnp.where(block_id >= step, pltpu.roll(upto, step, 0), 0)
        step *= 2
    ahead = upto - active
    rank = jnp.where(active > 0, ahead, upto[31:32] + block_id - ahead)
    order = jnp.sum(jnp.where(rank == lane_id, block_id, 0), axis=0, keepdims=True)
    slots = [order[0, k] for k in range(CAP)]

    load[1].wait()
    load[2].wait()

    def add_squares(c, total):
        x = tok[:, place(c)].astype(F32)
        return total + x * x

    squares = lax.fori_loop(
        0, features // LANES, add_squares, jnp.zeros((seqs, LANES), F32), unroll=8
    )
    scale = lax.rsqrt(jnp.sum(squares, axis=1, keepdims=True) / features + EPS)
    mine = (tok[:, place(hot)].astype(F32) * scale * gain[:, place(hot)]).astype(BF16)

    load[3].wait()
    load[4].wait()
    for k in range(CAP):
        cols = pl.ds(slots[k] * LANES, LANES)
        both = jnp.concatenate([cg[:, cols], cu[:, cols]], axis=1)
        part = jnp.dot(mine, both, preferred_element_type=F32).astype(BF16)
        s1[k // 2, k % 2, 0] = part[:, :LANES]
        s1[k // 2, k % 2, 1] = part[:, LANES:]

    @pl.when(adds)
    def _():
        pl.semaphore_wait(barrier, 45)

    @pl.when(core == 0)
    def _():
        pl.semaphore_wait(barrier, 23)

    def plane_copies(op):
        for k in (*FAR_PLANE, 0):
            to = in_plane_at(k)[0]
            sends = swap(core, to) < PAIRS
            if k == 0:
                sends = jnp.logical_and(sends, core == 0)
            op(k, to, sends)

    def s1_copy(k, to):
        return remote(
            s1.at[pair_of(core, to)],
            r1.at[core, p],
            s1_send.at[k],
            s1_recv.at[core, p],
            in_plane(to),
            partner,
        )

    def start_s1(k, to, sends):
        @pl.when(sends)
        def _():
            s1_copy(k, to).start()

    plane_copies(start_s1)

    def z_copies(op):
        for k in FAR_Z:
            op(k)

        @pl.when(core == 0)
        def _():
            op(0)

    def hd_copy(k):
        to = ring(z, k)
        return remote(
            hd_hbm.at[:, columns_of(to)],
            hdp.at[core, z],
            hd_send.at[k],
            hd_recv.at[core, z],
            along_z(to),
            partner,
        )

    z_copies(lambda k: hd_copy(k).start())

    load[5].wait()
    load[6].wait()

    def hot_chunk(c, total):
        cols = pl.ds(pl.multiple_of(c * CHUNK, CHUNK), CHUNK)
        normed = (tok[:, cols].astype(F32) * scale * gain[:, cols]).astype(BF16)
        return total + lax.dot_general(
            hw[:, cols], normed, (((1,), (1,)), ((), ())), preferred_element_type=F32
        )

    hot_t = lax.fori_loop(
        0, features // CHUNK, hot_chunk, jnp.zeros((32, seqs), F32)
    )
    hidden_t = silu(hot_t[:16]) * hot_t[16:]
    hh[core, z] = jnp.concatenate([hidden_t, jnp.zeros_like(hidden_t)], axis=1).astype(
        BF16
    )

    def hh_copy(k):
        return remote(
            hh.at[core, z],
            hh.at[core, z],
            hh_send.at[k],
            hh_recv.at[core, z],
            along_z(ring(z, k)),
            partner,
        )

    z_copies(lambda k: hh_copy(k).start())

    half = lax.rem(z, 2)
    rows = lax.div(z, 2)
    slot_own = pair_of(core, p) * 2 + half
    block_own = jnp.int32(0)
    for k in range(CAP):
        block_own = jnp.where(slot_own == k, slots[k], block_own)
    load[7].wait()
    unit = (cold * blocks_here + block_own) * LANES + lax.broadcasted_iota(
        jnp.int32, (LANES, LANES), 0
    )

    def match(c, found):
        return jnp.where(hidx[:, place(c)] == unit, 1.0, found)

    found = lax.fori_loop(
        0, hidx.shape[1] // LANES, match, jnp.zeros((LANES, LANES), F32), unroll=4
    )
    hot_units = lax.dot_general(
        jnp.ones((8, LANES), BF16),
        found.astype(BF16),
        (((1,), (1,)), ((), ())),
        preferred_element_type=F32,
    )[0:1]
    chosen = jnp.sum(
        jnp.where(block_id == block_own, mpad[...], 0).astype(F32), axis=0, keepdims=True
    )
    row = lax.broadcasted_iota(jnp.int32, (16, LANES), 0) + rows * 16
    column = lax.broadcasted_iota(jnp.int32, (16, LANES), 1)
    seq_live = jnp.sum(jnp.where(row == column, chosen, 0.0), axis=1, keepdims=True)
    lv[core] = (seq_live * (1.0 - jnp.minimum(hot_units, 1.0))).astype(BF16)
    lv_copy = remote(lv.at[0], lv.at[0], lv_send, lv_recv, hot, partner)

    @pl.when(core == 0)
    def _():
        lv_copy.start()

    load[8].wait()
    for k in range(CAP):
        block = cd[pl.ds(slots[k] * LANES, LANES), :]
        cds[k // 2, :, LANES * (k % 2) : LANES * (k % 2) + LANES] = jnp.transpose(block)

    def cd_copy(k, to):
        return remote(
            cds.at[pair_of(core, to)],
            cdr.at[core, p],
            cd_send.at[k],
            cd_recv.at[core, p],
            in_plane(to),
            partner,
        )

    def start_cd(k, to, sends):
        @pl.when(sends)
        def _():
            cd_copy(k, to).start()

    def s2_copy(group, k):
        to = ring(z, k)
        return remote(
            s2.at[group, to],
            r2.at[group, z],
            s2_send.at[group, k],
            s2_recv.at[group, z],
            along_z(to),
            partner,
        )

    piece = half * 4 + rows

    def h3_copy(group, k):
        return remote(
            h3.at[group, piece],
            h3.at[group, piece],
            h3_send.at[group, k],
            h3_recv.at[group, z],
            along_z(ring(z, k)),
            partner,
        )

    def fs_copy(k, other, core_to):
        cold_to = lax.rem(x_hi + other, 2) * 2 + core_to
        return remote(
            fs.at[4 * k + cold_to],
            fr.at[2 * k + other],
            fs_send,
            fs_recv,
            in_plane(in_plane_at(k)[0]),
            cold_to,
        )

    @pl.when(core == 0)
    def _():
        plane_copies(start_cd)

    @pl.when(adds)
    def _():
        for group in (1, 0):

            @pl.when(works(group))
            def _():
                if group:
                    total = s1[pair_of(1, p)].astype(F32)
                else:
                    total = jnp.zeros(s1.shape[1:], F32)
                for k in range(group, RING):
                    src = in_plane_at(k)[1]
                    remote(
                        s1.at[0],
                        r1.at[group, src],
                        s1_send.at[k],
                        s1_recv.at[group, src],
                        hot,
                        partner,
                    ).wait_recv()
                    total = total + r1[group, src].astype(F32)
                total = total.astype(BF16)
                for r in range(4):
                    for e in range(2):
                        for g in range(2):
                            s2[group, 2 * r + e, g] = total[e, g, 16 * r : 16 * r + 16]
                for k in FAR_Z:
                    s2_copy(group, k).start()

        plane_copies(start_cd)
        cdr[1, p] = cds[pair_of(1, p)]

        remote(lv.at[0], lv.at[0], lv_send, lv_recv, hot, partner).wait_recv()
        for group in (1, 0):

            @pl.when(works(group))
            def _():
                both = s2[group, z].astype(F32)
                for k in range(1, RING):
                    src = ring(z, k)
                    remote(
                        s2.at[group, src],
                        r2.at[group, src],
                        s2_send.at[group, k],
                        s2_recv.at[group, src],
                        hot,
                        partner,
                    ).wait_recv()
                    both = both + r2[group, src].astype(F32)
                live = lv[group].astype(F32)
                h3[group, piece] = (silu(both[0]) * both[1] * live).astype(BF16)
                for k in FAR_Z:
                    h3_copy(group, k).start()

        own_piece.wait()
        for group in range(2):
            for k in range(group, RING):
                src = ring(z, k)
                remote(
                    hdp.at[group, src],
                    hdp.at[group, src],
                    hd_send.at[k],
                    hd_recv.at[group, src],
                    hot,
                    partner,
                ).wait_recv()
                remote(
                    hh.at[group, src],
                    hh.at[group, src],
                    hh_send.at[k],
                    hh_recv.at[group, src],
                    hot,
                    partner,
                ).wait_recv()
        hidden = hh[...].reshape(2 * LANES, LANES)[:, :seqs]
        for q in range(RING):
            down = hdp[:, :, :, LANES * q : LANES * q + LANES].reshape(2 * LANES, LANES)
            acc[q] = jnp.dot(jnp.transpose(down), hidden, preferred_element_type=F32)

        def await_pair(group):
            @pl.when(works(group))
            def _():
                for k in range(group, RING):
                    src = in_plane_at(k)[1]
                    remote(
                        cds.at[0],
                        cdr.at[group, src],
                        cd_send.at[k],
                        cd_recv.at[group, src],
                        hot,
                        partner,
                    ).wait_recv()
                for k in range(1, RING):
                    src = ring(z, k)
                    remote(
                        h3.at[group, piece],
                        h3.at[group, piece],
                        h3_send.at[group, k],
                        h3_recv.at[group, src],
                        hot,
                        partner,
                    ).wait_recv()

        def pair_hidden(group):
            return jnp.concatenate(
                [
                    h3[group, 0:4].reshape(seqs, LANES),
                    h3[group, 4:8].reshape(seqs, LANES),
                ],
                axis=1,
            )

        def pair_term(group, values, to):
            term = lax.dot_general(
                cdr[group, to],
                values,
                (((1,), (1,)), ((), ())),
                preferred_element_type=F32,
            )
            return acc[to] + jnp.where(works(group), term, 0.0)

        await_pair(1)
        values = pair_hidden(1)
        for q in range(RING):
            acc[q] = pair_term(1, values, q)
        await_pair(0)

        values = pair_hidden(0)
        terms = [pair_term(0, values, in_plane_at(k)[0]) for k in (*FAR_PLANE, 0)]
        for k, term in zip((*FAR_PLANE, 0), terms):
            for c in range(4):
                fs[4 * k + c] = jnp.concatenate(
                    [term[32 * c : 32 * c + 16], term[32 * c + 16 : 32 * c + 32]], axis=1
                ).astype(BF16)
            for other, core_to in ((1, 0), (1, 1), (0, 0), (0, 1)):
                if k + other or not core_to:
                    fs_copy(k, other, core_to).start()

        fr[0] = fs[cold]

    @pl.when(adds)
    def _():
        landed = fr.at[pl.ds(1, 2 * RING - 1)]
        pltpu.make_async_copy(landed, landed, fs_recv).wait()

    @pl.when(core == 0)
    def _():
        pltpu.make_async_copy(fr, fr, fs_recv).wait()

    result = fr[0].astype(F32)
    for i in range(1, 2 * RING):
        result = result + fr[i].astype(F32)
    out_ref[0:16, :] = result[:, :seqs].astype(BF16)
    out_ref[16:32, :] = result[:, seqs:].astype(BF16)

    def drain(k, to, sends):
        @pl.when(sends)
        def _():
            s1_copy(k, to).wait_send()
            cd_copy(k, to).wait_send()

    plane_copies(drain)
    z_copies(lambda k: hd_copy(k).wait_send())
    z_copies(lambda k: hh_copy(k).wait_send())

    @pl.when(core == 0)
    def _():
        lv_copy.wait_send()

    @pl.when(adds)
    def _():
        for group in range(2):

            @pl.when(works(group))
            def _():
                for k in FAR_Z:
                    s2_copy(group, k).wait_send()
                    h3_copy(group, k).wait_send()

        sent = fs.at[pl.ds(0, 4 * RING - 1)]
        pltpu.make_async_copy(sent, sent, fs_send).wait()


def on_device(
    tokens,
    norm_gain,
    hot_gate,
    hot_up,
    hot_down,
    hot_index,
    cold_gate,
    cold_up,
    cold_down,
    block_mask,
):
    seqs, features = tokens.shape
    dma = pltpu.SemaphoreType.DMA
    any_space = pl.BlockSpec(memory_space=pl.ANY)
    return pl.pallas_call(
        kernel,
        out_shape=jax.ShapeDtypeStruct((32, seqs), BF16),
        in_specs=[any_space] * 10,
        out_specs=pl.BlockSpec(memory_space=pltpu.VMEM),
        scratch_shapes=[
            pltpu.VMEM(tokens.shape, BF16),
            pltpu.VMEM((1, features), F32),
            pltpu.VMEM((32, features), BF16),
            pltpu.VMEM((1, hot_index.shape[0]), jnp.int32),
            pltpu.VMEM(cold_gate.shape, BF16),
            pltpu.VMEM(cold_up.shape, BF16),
            pltpu.VMEM(cold_down.shape, BF16),
            pltpu.VMEM(block_mask.shape[::-1], jnp.int32),
            pltpu.VMEM((32, LANES), jnp.int32),
            pltpu.VMEM((PAIRS, 2, 2, seqs, LANES), BF16),
            pltpu.VMEM((2, RING, 2, 2, seqs, LANES), BF16),
            pltpu.VMEM((2, RING, 2, 16, LANES), BF16),
            pltpu.VMEM((2, RING, 2, 16, LANES), BF16),
            pltpu.VMEM((2, RING, 16, LANES), BF16),
            pltpu.VMEM((PAIRS, LANES, 2 * LANES), BF16),
            pltpu.VMEM((2, RING, LANES, 2 * LANES), BF16),
            pltpu.VMEM((2, RING, 16, RING * LANES), BF16),
            pltpu.VMEM((2, RING, 16, LANES), BF16),
            pltpu.VMEM((2, 16, LANES), BF16),
            pltpu.VMEM((RING, LANES, seqs), F32),
            pltpu.VMEM((RING * 4, 16, LANES), BF16),
            pltpu.VMEM((2 * RING, 16, LANES), BF16),
            dma((9,)),
            dma((1,)),
            dma((RING,)),
            dma((2, RING)),
            dma((2, RING)),
            dma((2, RING)),
            dma((2, RING)),
            dma((2, RING)),
            dma((RING,)),
            dma((2, RING)),
            dma((RING,)),
            dma((2, RING)),
            dma((RING,)),
            dma((2, RING)),
            dma,
            dma,
            dma,
            dma,
        ],
        compiler_params=pltpu.CompilerParams(
            collective_id=0, has_side_effects=True, vmem_limit_bytes=55218 * 1024
        ),
    )(
        tokens,
        norm_gain.reshape(1, -1),
        hot_gate,
        hot_up,
        hot_down,
        hot_index.reshape(1, -1),
        cold_gate,
        cold_up,
        cold_down,
        block_mask.T,
    ).T


def solution(mesh):
    rows = P(("hot", "cold"), None)
    return jax.shard_map(
        on_device,
        mesh=mesh,
        in_specs=(
            P(),
            P(),
            rows,
            rows,
            rows,
            P(),
            P("hot", "cold"),
            P("hot", "cold"),
            P("cold", "hot"),
            P(None, "cold"),
        ),
        out_specs=P(None, ("hot", "cold")),
        check_vma=False,
    )
```

time: 38.7 us -> 34.9 us (0.902)
  Pallas kernels: 37.2 us -> 34.1 us
  local copies, waits for them, and re-layouts: 1.3 us -> 0.6 us
    pallas_call x1, Pallas kernels: 37.2 us -> 34.1 us  [on_device(): pl.pallas_call(kernel, out_shape=jax.ShapeDtypeStruct((32, seqs), BF16),...]
    unnamed x1, local copies, waits for them, and re-layouts: 1.3 us -> 0.6 us
where the time goes in v3:
time: 34.9 us; the launch traced here: 34.8 us
  Pallas kernels  34.1 us (98%)
  local copies, waits for them, and re-layouts  0.6 us (2%)
    pallas_call x1, Pallas kernels, on_device(): pl.pallas_call(kernel, out_shape=jax.ShapeDtypeStruct((32, seqs), BF16),...  34.1 us

profile of v3, /device:TPU:1, one launch (start us, length us, event | category | flops | bytes accessed | tf_op | source)
XLA Modules:
  0.0 34.8 jit_solution(1866003900400769342)
XLA Ops:
  0.0 34.1 %shard_map.100 = bf16[32,64]{1,0:T(8,128)(2,1)S(1)} custom-call(bf16[64,8192]{1,0:T(8,128)(2,1)} %tok_hbm.1, f32[1,8192]{1,0:T(1,128)} %bitcast.5, bf16[16,8192]{1,0:T(8,128)(2,1)} %hg_hbm.1, bf16[16,8192]{1,0:T(8,128)(2,1)} %hu_hbm.1, bf16[16,8192]{1,0:T(8,128)(2,1)} %hd_hbm.1, s32[1,4096]{1,0:T(1,128)} %bitcast.6, bf16[128,3584]{1,0:T(8,128)(2,1)} %cg_hbm.1, ...), custom_call_target="tpu_custom_call" | custom-call | tf_op jit(solution)/shard_map/pallas_call | solution.py:603
  34.2 0.6 %copy.12 = bf16[64,32]{0,1:T(8,128)(2,1)} copy(bf16[64,32]{0,1:T(8,128)(2,1)S(1)} %bitcast.4) | data formatting | bytes 8192

commit v4 on v3

--- a/solution.py
+++ b/solution.py
@@ -13,6 +13,10 @@
 RING = 8
 FAR_Z = (4, 3, 5, 2, 6, 1, 7)
 FAR_PLANE = (5, 4, 3, 7, 2, 6, 1)
+NEAR_PLANE = (1, 2, 6, 3, 7, 4, 5)
+EARLY_Z = (4, 2, 6)
+LATE_Z = (3, 5, 1, 7)
+Z_FIRST = 2
 PAIRS = 7
 CAP = 14
 LANES = 128
@@ -44,13 +48,14 @@
     gain,
     hw,
     hidx,
-    cg,
-    cu,
+    cgu,
     cd,
     msk,
     mpad,
     s1,
     r1,
+    rb,
+    sq,
     s2,
     r2,
     h3,
@@ -63,11 +68,13 @@
     fs,
     fr,
     load_sem,
-    own_sem,
     s1_send,
     s1_recv,
+    sb_send,
+    sb_recv,
+    sq_send,
     s2_send,
-    s2_recv,
+    r2_recv,
     h3_send,
     h3_recv,
     cd_send,
@@ -78,6 +85,7 @@
     hh_recv,
     lv_send,
     lv_recv,
+    go,
     fs_send,
     fs_recv,
 ):
@@ -103,7 +111,7 @@
         )
 
     def swap(group, place_or_pair):
-        return place_or_pair + group * (1 - 2 * lax.rem(place_or_pair, 2))
+        return 7 - place_or_pair + group * (2 * place_or_pair - 7)
 
     def works(group):
         return swap(group, p) < PAIRS
@@ -121,6 +129,9 @@
             device_id_type=MESH,
         )
 
+    def landed(ref, sem):
+        pltpu.make_async_copy(ref, ref, sem).wait()
+
     def in_plane(to):
         return z * RING + to
 
@@ -128,28 +139,24 @@
         return to * RING + p
 
     loads = [
-        (mask_hbm, msk),
-        (tok_hbm, tok),
-        (gain_hbm, gain),
-        (cg_hbm, cg),
-        (cu_hbm, cu),
-        (hg_hbm, hw.at[pl.ds(0, 16)]),
-        (hu_hbm, hw.at[pl.ds(16, 16)]),
-        (hidx_hbm, hidx),
-        (cd_hbm, cd),
+        (mask_hbm, msk, 0),
+        (tok_hbm, tok, 1),
+        (gain_hbm, gain, 2),
+        (cg_hbm, cgu.at[0], 3),
+        (cu_hbm, cgu.at[1], 3),
+        (hg_hbm, hw.at[pl.ds(0, 16)], 4),
+        (hu_hbm, hw.at[pl.ds(16, 16)], 4),
+        (hidx_hbm, hidx, 5),
+        (cd_hbm, cd, 6),
     ]
-    load = [
-        pltpu.make_async_copy(src, dst, load_sem.at[i])
-        for i, (src, dst) in enumerate(loads)
-    ]
-    for copy in load:
-        copy.start()
+    for src, dst, sem in loads:
+        pltpu.make_async_copy(src, dst, load_sem.at[sem]).start()
 
     def columns_of(zz):
         return pl.ds(pl.multiple_of(zz * RING * LANES, RING * LANES), RING * LANES)
 
     own_piece = pltpu.make_async_copy(
-        hd_hbm.at[:, columns_of(z)], hdp.at[1, z], own_sem.at[0]
+        hd_hbm.at[:, columns_of(z)], hdp.at[RING + z], load_sem.at[7]
     )
 
     @pl.when(adds)
@@ -182,7 +189,7 @@
     def _():
         greet(hot, partner)
 
-    load[0].wait()
+    landed(msk, load_sem.at[0])
     mpad[...] = jnp.zeros_like(mpad)
     mpad[0:blocks_here, 0:seqs] = msk[...]
     block_id = lax.broadcasted_iota(jnp.int32, mpad.shape, 0)
@@ -202,8 +209,8 @@
     order = jnp.sum(jnp.where(rank == lane_id, block_id, 0), axis=0, keepdims=True)
     slots = [order[0, k] for k in range(CAP)]
 
-    load[1].wait()
-    load[2].wait()
+    landed(tok, load_sem.at[1])
+    landed(gain, load_sem.at[2])
 
     def add_squares(c, total):
         x = tok[:, place(c)].astype(F32)
@@ -215,14 +222,16 @@
     scale = lax.rsqrt(jnp.sum(squares, axis=1, keepdims=True) / features + EPS)
     mine = (tok[:, place(hot)].astype(F32) * scale * gain[:, place(hot)]).astype(BF16)
 
-    load[3].wait()
-    load[4].wait()
+    landed(cgu, load_sem.at[3])
     for k in range(CAP):
         cols = pl.ds(slots[k] * LANES, LANES)
-        both = jnp.concatenate([cg[:, cols], cu[:, cols]], axis=1)
+        both = jnp.concatenate([cgu[0, :, cols], cgu[1, :, cols]], axis=1)
         part = jnp.dot(mine, both, preferred_element_type=F32).astype(BF16)
-        s1[k // 2, k % 2, 0] = part[:, :LANES]
-        s1[k // 2, k % 2, 1] = part[:, LANES:]
+        pair, half = divmod(k, 2)
+        for r in range(4):
+            at = (2 * r + half - pair) % RING
+            s1[pair, at, 0] = part[16 * r : 16 * r + 16, :LANES]
+            s1[pair, at, 1] = part[16 * r : 16 * r + 16, LANES:]
 
     @pl.when(adds)
     def _():
@@ -232,8 +241,8 @@
     def _():
         pl.semaphore_wait(barrier, 23)
 
-    def plane_copies(op):
-        for k in (*FAR_PLANE, 0):
+    def plane_copies(order, op):
+        for k in (*order, 0):
             to = in_plane_at(k)[0]
             sends = swap(core, to) < PAIRS
             if k == 0:
@@ -242,10 +251,10 @@
 
     def s1_copy(k, to):
         return remote(
-            s1.at[pair_of(core, to)],
+            s1.at[pair_of(core, to), pl.ds(Z_FIRST, RING - Z_FIRST)],
             r1.at[core, p],
-            s1_send.at[k],
-            s1_recv.at[core, p],
+            s1_send,
+            s1_recv.at[core],
             in_plane(to),
             partner,
         )
@@ -255,31 +264,55 @@
         def _():
             s1_copy(k, to).start()
 
-    plane_copies(start_s1)
-
-    def z_copies(op):
-        for k in FAR_Z:
+    plane_copies(NEAR_PLANE, start_s1)
+
+    def z_copies(order, op):
+        for k in order:
             op(k)
 
         @pl.when(core == 0)
         def _():
             op(0)
+
+    def pair_at(zz, b):
+        return lax.rem(zz + RING - b, RING)
+
+    def sb_copies(op):
+        def each(k):
+            to = ring(z, k)
+            for b in range(Z_FIRST):
+                pair = pair_at(to, b)
+                copy = remote(
+                    s1.at[jnp.minimum(pair, PAIRS - 1), b],
+                    rb.at[core, b, z],
+                    sb_send,
+                    sb_recv.at[core, b],
+                    along_z(to),
+                    partner,
+                )
+
+                @pl.when(pair < PAIRS)
+                def _():
+                    op(copy)
+
+        z_copies(FAR_Z, each)
+
+    sb_copies(lambda copy: copy.start())
 
     def hd_copy(k):
         to = ring(z, k)
         return remote(
             hd_hbm.at[:, columns_of(to)],
-            hdp.at[core, z],
-            hd_send.at[k],
-            hd_recv.at[core, z],
+            hdp.at[core * RING + z],
+            hd_send,
+            hd_recv,
             along_z(to),
             partner,
         )
 
-    z_copies(lambda k: hd_copy(k).start())
-
-    load[5].wait()
-    load[6].wait()
+    z_copies(EARLY_Z, lambda k: hd_copy(k).start())
+
+    landed(hw, load_sem.at[4])
 
     def hot_chunk(c, total):
         cols = pl.ds(pl.multiple_of(c * CHUNK, CHUNK), CHUNK)
@@ -292,21 +325,21 @@
         0, features // CHUNK, hot_chunk, jnp.zeros((32, seqs), F32)
     )
     hidden_t = silu(hot_t[:16]) * hot_t[16:]
-    hh[core, z] = jnp.concatenate([hidden_t, jnp.zeros_like(hidden_t)], axis=1).astype(
+    hh[core * RING + z] = jnp.concatenate([hidden_t, jnp.zeros_like(hidden_t)], axis=1).astype(
         BF16
     )
 
     def hh_copy(k):
         return remote(
-            hh.at[core, z],
-            hh.at[core, z],
-            hh_send.at[k],
-            hh_recv.at[core, z],
+            hh.at[core * RING + z],
+            hh.at[core * RING + z],
+            hh_send,
+            hh_recv,
             along_z(ring(z, k)),
             partner,
         )
 
-    z_copies(lambda k: hh_copy(k).start())
+    z_copies(FAR_Z, lambda k: hh_copy(k).start())
 
     half = lax.rem(z, 2)
     rows = lax.div(z, 2)
@@ -314,7 +347,7 @@
     block_own = jnp.int32(0)
     for k in range(CAP):
         block_own = jnp.where(slot_own == k, slots[k], block_own)
-    load[7].wait()
+    landed(hidx, load_sem.at[5])
     unit = (cold * blocks_here + block_own) * LANES + lax.broadcasted_iota(
         jnp.int32, (LANES, LANES), 0
     )
@@ -344,7 +377,7 @@
     def _():
         lv_copy.start()
 
-    load[8].wait()
+    landed(cd, load_sem.at[6])
     for k in range(CAP):
         block = cd[pl.ds(slots[k] * LANES, LANES), :]
         cds[k // 2, :, LANES * (k % 2) : LANES * (k % 2) + LANES] = jnp.transpose(block)
@@ -353,8 +386,8 @@
         return remote(
             cds.at[pair_of(core, to)],
             cdr.at[core, p],
-            cd_send.at[k],
-            cd_recv.at[core, p],
+            cd_send,
+            cd_recv.at[core],
             in_plane(to),
             partner,
         )
@@ -364,14 +397,36 @@
         def _():
             cd_copy(k, to).start()
 
-    def s2_copy(group, k):
-        to = ring(z, k)
-        return remote(
-            s2.at[group, to],
-            r2.at[group, z],
-            s2_send.at[group, k],
-            s2_recv.at[group, z],
-            along_z(to),
+    def s2_copies(group, op, own=None):
+        for at in range(Z_FIRST, RING):
+            to = lax.rem(pair_of(group, p) + at, RING)
+            copy = remote(
+                s2.at[group, at - Z_FIRST],
+                r2.at[group * RING + z],
+                s2_send.at[group],
+                r2_recv.at[group],
+                along_z(to),
+                partner,
+            )
+
+            @pl.when(to != z)
+            def _():
+                op(copy)
+
+            if own is not None:
+
+                @pl.when(to == z)
+                def _():
+                    own(at - Z_FIRST)
+
+    def sq_copy(group, b):
+        to = swap(group, pair_at(z, b))
+        return to, remote(
+            sq.at[group, b],
+            r2.at[group * RING + p],
+            sq_send.at[group, b],
+            r2_recv.at[group],
+            in_plane(jnp.maximum(to, 0)),
             partner,
         )
 
@@ -381,8 +436,8 @@
         return remote(
             h3.at[group, piece],
             h3.at[group, piece],
-            h3_send.at[group, k],
-            h3_recv.at[group, z],
+            h3_send.at[group],
+            h3_recv.at[group],
             along_z(ring(z, k)),
             partner,
         )
@@ -400,38 +455,62 @@
 
     @pl.when(core == 0)
     def _():
-        plane_copies(start_cd)
+        pl.semaphore_wait(go, 1)
+        for k in LATE_Z:
+            hd_copy(k).start()
+        plane_copies(FAR_PLANE, start_cd)
 
     @pl.when(adds)
     def _():
+        for group in (1, 0):
+            for b in range(Z_FIRST):
+                pair = pair_at(z, b)
+
+                @pl.when(pair < PAIRS)
+                def _():
+                    if group:
+                        total = s1[jnp.minimum(pair, PAIRS - 1), b].astype(F32)
+                    else:
+                        total = jnp.zeros(s1.shape[2:], F32)
+                    landed(rb.at[group, b, pl.ds(0, RING - group)], sb_recv.at[group, b])
+                    for k in range(group, RING):
+                        total = total + rb[group, b, ring(z, k)].astype(F32)
+                    sq[group, b] = total.astype(BF16)
+                    to, copy = sq_copy(group, b)
+
+                    @pl.when(to != p)
+                    def _():
+                        copy.start()
+
+                    @pl.when(to == p)
+                    def _():
+                        r2[group * RING + p] = sq[group, b]
+
         for group in (1, 0):
 
             @pl.when(works(group))
             def _():
                 if group:
-                    total = s1[pair_of(1, p)].astype(F32)
+                    total = s1[pair_of(1, p), Z_FIRST:].astype(F32)
                 else:
-                    total = jnp.zeros(s1.shape[1:], F32)
+                    total = jnp.zeros((RING - Z_FIRST, *s1.shape[2:]), F32)
+                landed(r1.at[group, pl.ds(0, RING - group)], s1_recv.at[group])
                 for k in range(group, RING):
-                    src = in_plane_at(k)[1]
-                    remote(
-                        s1.at[0],
-                        r1.at[group, src],
-                        s1_send.at[k],
-                        s1_recv.at[group, src],
-                        hot,
-                        partner,
-                    ).wait_recv()
-                    total = total + r1[group, src].astype(F32)
-                total = total.astype(BF16)
-                for r in range(4):
-                    for e in range(2):
-                        for g in range(2):
-                            s2[group, 2 * r + e, g] = total[e, g, 16 * r : 16 * r + 16]
-                for k in FAR_Z:
-                    s2_copy(group, k).start()
-
-        plane_copies(start_cd)
+                    total = total + r1[group, ring(p, k)].astype(F32)
+                s2[group] = total.astype(BF16)
+
+                def own(at):
+                    r2[group * RING + z] = s2[group, at]
+
+                s2_copies(group, lambda copy: copy.start(), own)
+
+        pl.semaphore_signal(
+            go, inc=1, device_id=(hot, x_hi * 2), device_id_type=MESH
+        )
+
+        for k in LATE_Z:
+            hd_copy(k).start()
+        plane_copies(FAR_PLANE, start_cd)
         cdr[1, p] = cds[pair_of(1, p)]
 
         remote(lv.at[0], lv.at[0], lv_send, lv_recv, hot, partner).wait_recv()
@@ -439,71 +518,29 @@
 
             @pl.when(works(group))
             def _():
-                both = s2[group, z].astype(F32)
-                for k in range(1, RING):
-                    src = ring(z, k)
-                    remote(
-                        s2.at[group, src],
-                        r2.at[group, src],
-                        s2_send.at[group, k],
-                        s2_recv.at[group, src],
-                        hot,
-                        partner,
-                    ).wait_recv()
-                    both = both + r2[group, src].astype(F32)
+                pieces = r2.at[pl.ds(group * RING, RING)]
+                landed(pieces.at[pl.ds(0, RING - 1)], r2_recv.at[group])
+                both = pieces[0].astype(F32)
+                for i in range(1, RING):
+                    both = both + pieces[i].astype(F32)
                 live = lv[group].astype(F32)
                 h3[group, piece] = (silu(both[0]) * both[1] * live).astype(BF16)
                 for k in FAR_Z:
                     h3_copy(group, k).start()
 
         own_piece.wait()
-        for group in range(2):
-            for k in range(group, RING):
-                src = ring(z, k)
-                remote(
-                    hdp.at[group, src],
-                    hdp.at[group, src],
-                    hd_send.at[k],
-                    hd_recv.at[group, src],
-                    hot,
-                    partner,
-                ).wait_recv()
-                remote(
-                    hh.at[group, src],
-                    hh.at[group, src],
-                    hh_send.at[k],
-                    hh_recv.at[group, src],
-                    hot,
-                    partner,
-                ).wait_recv()
+        landed(hdp.at[pl.ds(0, 2 * RING - 1)], hd_recv)
+        landed(hh.at[pl.ds(0, 2 * RING - 1)], hh_recv)
         hidden = hh[...].reshape(2 * LANES, LANES)[:, :seqs]
         for q in range(RING):
-            down = hdp[:, :, :, LANES * q : LANES * q + LANES].reshape(2 * LANES, LANES)
+            down = hdp[:, :, LANES * q : LANES * q + LANES].reshape(2 * LANES, LANES)
             acc[q] = jnp.dot(jnp.transpose(down), hidden, preferred_element_type=F32)
 
         def await_pair(group):
             @pl.when(works(group))
             def _():
-                for k in range(group, RING):
-                    src = in_plane_at(k)[1]
-                    remote(
-                        cds.at[0],
-                        cdr.at[group, src],
-                        cd_send.at[k],
-                        cd_recv.at[group, src],
-                        hot,
-                        partner,
-                    ).wait_recv()
-                for k in range(1, RING):
-                    src = ring(z, k)
-                    remote(
-                        h3.at[group, piece],
-                        h3.at[group, piece],
-                        h3_send.at[group, k],
-                        h3_recv.at[group, src],
-                        hot,
-                        partner,
-                    ).wait_recv()
+                landed(cdr.at[group, pl.ds(0, RING - group)], cd_recv.at[group])
+                landed(h3.at[group, pl.ds(0, RING - 1)], h3_recv.at[group])
 
         def pair_hidden(group):
             return jnp.concatenate(
@@ -557,32 +594,62 @@
     out_ref[0:16, :] = result[:, :seqs].astype(BF16)
     out_ref[16:32, :] = result[:, seqs:].astype(BF16)
 
-    def drain(k, to, sends):
-        @pl.when(sends)
+    fewer = jnp.logical_and(adds, works(1))
+    ends = jnp.logical_or(z == 0, z == RING - 1)
+
+    @pl.when(fewer)
+    def _():
+        landed(r1.at[0, pl.ds(0, PAIRS - 1)], s1_send)
+        landed(cdr.at[0, pl.ds(0, PAIRS - 1)], cd_send)
+
+    @pl.when(jnp.logical_not(fewer))
+    def _():
+        landed(r1.at[0, pl.ds(0, PAIRS)], s1_send)
+        landed(cdr.at[0, pl.ds(0, PAIRS)], cd_send)
+
+    @pl.when(core == 0)
+    def _():
+        landed(r2.at[pl.ds(0, 14)], sb_send)
+        landed(hdp.at[pl.ds(0, RING)], hd_send)
+        landed(hh.at[pl.ds(0, RING)], hh_send)
+        lv_copy.wait_send()
+
+    @pl.when(adds)
+    def _():
+        landed(hdp.at[pl.ds(0, RING - 1)], hd_send)
+        landed(hh.at[pl.ds(0, RING - 1)], hh_send)
+
+        @pl.when(ends)
         def _():
-            s1_copy(k, to).wait_send()
-            cd_copy(k, to).wait_send()
-
-    plane_copies(drain)
-    z_copies(lambda k: hd_copy(k).wait_send())
-    z_copies(lambda k: hh_copy(k).wait_send())
-
-    @pl.when(core == 0)
-    def _():
-        lv_copy.wait_send()
-
-    @pl.when(adds)
-    def _():
+            landed(r2.at[pl.ds(0, 13)], sb_send)
+
+        @pl.when(jnp.logical_not(ends))
+        def _():
+            landed(r2.at[pl.ds(0, 12)], sb_send)
+
         for group in range(2):
+            z_first = lax.rem(z + RING - pair_of(group, p), RING) < Z_FIRST
+
+            @pl.when(jnp.logical_and(works(group), z_first))
+            def _():
+                landed(r2.at[pl.ds(0, RING - Z_FIRST)], s2_send.at[group])
+
+            @pl.when(jnp.logical_and(works(group), jnp.logical_not(z_first)))
+            def _():
+                landed(r2.at[pl.ds(0, RING - Z_FIRST - 1)], s2_send.at[group])
 
             @pl.when(works(group))
             def _():
-                for k in FAR_Z:
-                    s2_copy(group, k).wait_send()
-                    h3_copy(group, k).wait_send()
-
-        sent = fs.at[pl.ds(0, 4 * RING - 1)]
-        pltpu.make_async_copy(sent, sent, fs_send).wait()
+                landed(h3.at[group, pl.ds(0, RING - 1)], h3_send.at[group])
+
+            for b in range(Z_FIRST):
+                to, copy = sq_copy(group, b)
+
+                @pl.when(jnp.logical_and(pair_at(z, b) < PAIRS, to != p))
+                def _():
+                    copy.wait_send()
+
+        landed(fs.at[pl.ds(0, 4 * RING - 1)], fs_send)
 
 
 def on_device(
@@ -610,40 +677,44 @@
             pltpu.VMEM((1, features), F32),
             pltpu.VMEM((32, features), BF16),
             pltpu.VMEM((1, hot_index.shape[0]), jnp.int32),
-            pltpu.VMEM(cold_gate.shape, BF16),
-            pltpu.VMEM(cold_up.shape, BF16),
+            pltpu.VMEM((2, *cold_gate.shape), BF16),
             pltpu.VMEM(cold_down.shape, BF16),
             pltpu.VMEM(block_mask.shape[::-1], jnp.int32),
             pltpu.VMEM((32, LANES), jnp.int32),
-            pltpu.VMEM((PAIRS, 2, 2, seqs, LANES), BF16),
-            pltpu.VMEM((2, RING, 2, 2, seqs, LANES), BF16),
-            pltpu.VMEM((2, RING, 2, 16, LANES), BF16),
-            pltpu.VMEM((2, RING, 2, 16, LANES), BF16),
+            pltpu.VMEM((PAIRS, RING, 2, 16, LANES), BF16),
+            pltpu.VMEM((2, RING, RING - Z_FIRST, 2, 16, LANES), BF16),
+            pltpu.VMEM((2, Z_FIRST, RING, 2, 16, LANES), BF16),
+            pltpu.VMEM((2, Z_FIRST, 2, 16, LANES), BF16),
+            pltpu.VMEM((2, RING - Z_FIRST, 2, 16, LANES), BF16),
+            pltpu.VMEM((2 * RING, 2, 16, LANES), BF16),
             pltpu.VMEM((2, RING, 16, LANES), BF16),
             pltpu.VMEM((PAIRS, LANES, 2 * LANES), BF16),
             pltpu.VMEM((2, RING, LANES, 2 * LANES), BF16),
-            pltpu.VMEM((2, RING, 16, RING * LANES), BF16),
-            pltpu.VMEM((2, RING, 16, LANES), BF16),
+            pltpu.VMEM((2 * RING, 16, RING * LANES), BF16),
+            pltpu.VMEM((2 * RING, 16, LANES), BF16),
             pltpu.VMEM((2, 16, LANES), BF16),
             pltpu.VMEM((RING, LANES, seqs), F32),
             pltpu.VMEM((RING * 4, 16, LANES), BF16),
             pltpu.VMEM((2 * RING, 16, LANES), BF16),
-            dma((9,)),
-            dma((1,)),
-            dma((RING,)),
-            dma((2, RING)),
-            dma((2, RING)),
-            dma((2, RING)),
-            dma((2, RING)),
-            dma((2, RING)),
-            dma((RING,)),
-            dma((2, RING)),
-            dma((RING,)),
-            dma((2, RING)),
-            dma((RING,)),
-            dma((2, RING)),
-            dma,
-            dma,
+            dma((8,)),
+            dma,
+            dma((2,)),
+            dma,
+            dma((2, Z_FIRST)),
+            dma((2, Z_FIRST)),
+            dma((2,)),
+            dma((2,)),
+            dma((2,)),
+            dma((2,)),
+            dma,
+            dma((2,)),
+            dma,
+            dma,
+            dma,
+            dma,
+            dma,
+            dma,
+            pltpu.SemaphoreType.REGULAR,
             dma,
             dma,
         ],

time: 34.9 us -> 32.1 us (0.920)
  Pallas kernels: 34.1 us -> 31.4 us
    pallas_call x1, Pallas kernels: 34.1 us -> 31.4 us  [on_device(): pl.pallas_call(kernel, out_shape=jax.ShapeDtypeStruct((32, seqs), BF16),...]
where the time goes in v4:
time: 32.1 us; the launch traced here: 32 us
  Pallas kernels  31.4 us (98%)
  local copies, waits for them, and re-layouts  0.6 us (2%)
    pallas_call x1, Pallas kernels, on_device(): pl.pallas_call(kernel, out_shape=jax.ShapeDtypeStruct((32, seqs), BF16),...  31.4 us

profile of v4, /device:TPU:1, one launch (start us, length us, event | category | flops | bytes accessed | tf_op | source)
XLA Modules:
  0.0 32.0 jit_solution(3314912662942336934)
XLA Ops:
  0.0 31.4 %shard_map.100 = bf16[32,64]{1,0:T(8,128)(2,1)S(1)} custom-call(bf16[64,8192]{1,0:T(8,128)(2,1)} %tok_hbm.1, f32[1,8192]{1,0:T(1,128)} %bitcast.5, bf16[16,8192]{1,0:T(8,128)(2,1)} %hg_hbm.1, bf16[16,8192]{1,0:T(8,128)(2,1)} %hu_hbm.1, bf16[16,8192]{1,0:T(8,128)(2,1)} %hd_hbm.1, s32[1,4096]{1,0:T(1,128)} %bitcast.6, bf16[128,3584]{1,0:T(8,128)(2,1)} %cg_hbm.1, ...), custom_call_target="tpu_custom_call" | custom-call | tf_op jit(solution)/shard_map/pallas_call | solution.py:670
  31.4 0.6 %copy.12 = bf16[64,32]{0,1:T(8,128)(2,1)} copy(bf16[64,32]{0,1:T(8,128)(2,1)S(1)} %bitcast.4) | data formatting | bytes 8192

commit v5 on v4

--- a/solution.py
+++ b/solution.py
@@ -12,11 +12,9 @@
 BF16 = jnp.bfloat16
 RING = 8
 FAR_Z = (4, 3, 5, 2, 6, 1, 7)
+NEAR_Z = (2, 6, 1, 7)
+BEYOND_Z = (4, 3, 5)
 FAR_PLANE = (5, 4, 3, 7, 2, 6, 1)
-NEAR_PLANE = (1, 2, 6, 3, 7, 4, 5)
-EARLY_Z = (4, 2, 6)
-LATE_Z = (3, 5, 1, 7)
-Z_FIRST = 2
 PAIRS = 7
 CAP = 14
 LANES = 128
@@ -54,8 +52,6 @@
     mpad,
     s1,
     r1,
-    rb,
-    sq,
     s2,
     r2,
     h3,
@@ -68,16 +64,12 @@
     fs,
     fr,
     load_sem,
-    s1_send,
+    plane_send,
     s1_recv,
-    sb_send,
-    sb_recv,
-    sq_send,
     s2_send,
     r2_recv,
     h3_send,
     h3_recv,
-    cd_send,
     cd_recv,
     hd_send,
     hd_recv,
@@ -86,6 +78,8 @@
     lv_send,
     lv_recv,
     go,
+    zgo,
+    xgo,
     fs_send,
     fs_recv,
 ):
@@ -170,20 +164,19 @@
             barrier, inc=1, device_id=(hot_to, cold_to), device_id_type=MESH
         )
 
-    for k in FAR_Z:
-        greet(along_z(ring(z, k)), partner)
+    other_x = (1 - x_hi) * 2 + 1
     for k in FAR_PLANE:
         greet(in_plane(in_plane_at(k)[0]), partner)
-        greet(in_plane(in_plane_at(k)[0]), (1 - x_hi) * 2 + 1)
-    greet(hot, (1 - x_hi) * 2 + 1)
+    for k in NEAR_Z:
+        greet(along_z(ring(z, k)), partner)
 
     @pl.when(adds)
     def _():
-        for k in FAR_Z:
-            greet(along_z(ring(z, k)), x_hi * 2)
         for k in (*FAR_PLANE, 0):
             greet(in_plane(in_plane_at(k)[0]), x_hi * 2)
-            greet(in_plane(in_plane_at(k)[0]), (1 - x_hi) * 2)
+        for k in NEAR_Z:
+            greet(along_z(ring(z, k)), x_hi * 2)
+        greet(hot, other_x)
 
     @pl.when(core == 0)
     def _():
@@ -227,19 +220,27 @@
         cols = pl.ds(slots[k] * LANES, LANES)
         both = jnp.concatenate([cgu[0, :, cols], cgu[1, :, cols]], axis=1)
         part = jnp.dot(mine, both, preferred_element_type=F32).astype(BF16)
-        pair, half = divmod(k, 2)
         for r in range(4):
-            at = (2 * r + half - pair) % RING
-            s1[pair, at, 0] = part[16 * r : 16 * r + 16, :LANES]
-            s1[pair, at, 1] = part[16 * r : 16 * r + 16, LANES:]
+            at = 2 * r + k % 2
+            s1[k // 2, at, 0] = part[16 * r : 16 * r + 16, :LANES]
+            s1[k // 2, at, 1] = part[16 * r : 16 * r + 16, LANES:]
 
     @pl.when(adds)
     def _():
-        pl.semaphore_wait(barrier, 45)
+        pl.semaphore_wait(barrier, 24)
+        for k in (2, 6):
+            for core_to in range(2):
+                pl.semaphore_signal(
+                    zgo,
+                    inc=1,
+                    device_id=(along_z(ring(z, k)), x_hi * 2 + core_to),
+                    device_id_type=MESH,
+                )
+        pl.semaphore_signal(xgo, inc=1, device_id=(hot, other_x), device_id_type=MESH)
 
     @pl.when(core == 0)
     def _():
-        pl.semaphore_wait(barrier, 23)
+        pl.semaphore_wait(barrier, 12)
 
     def plane_copies(order, op):
         for k in (*order, 0):
@@ -251,9 +252,9 @@
 
     def s1_copy(k, to):
         return remote(
-            s1.at[pair_of(core, to), pl.ds(Z_FIRST, RING - Z_FIRST)],
-            r1.at[core, p],
-            s1_send,
+            s1.at[pair_of(core, to)],
+            r1.at[core * RING + p],
+            plane_send,
             s1_recv.at[core],
             in_plane(to),
             partner,
@@ -264,40 +265,14 @@
         def _():
             s1_copy(k, to).start()
 
-    plane_copies(NEAR_PLANE, start_s1)
+    plane_copies(FAR_PLANE, start_s1)
 
     def z_copies(order, op):
         for k in order:
-            op(k)
-
-        @pl.when(core == 0)
-        def _():
-            op(0)
-
-    def pair_at(zz, b):
-        return lax.rem(zz + RING - b, RING)
-
-    def sb_copies(op):
-        def each(k):
-            to = ring(z, k)
-            for b in range(Z_FIRST):
-                pair = pair_at(to, b)
-                copy = remote(
-                    s1.at[jnp.minimum(pair, PAIRS - 1), b],
-                    rb.at[core, b, z],
-                    sb_send,
-                    sb_recv.at[core, b],
-                    along_z(to),
-                    partner,
-                )
-
-                @pl.when(pair < PAIRS)
-                def _():
-                    op(copy)
-
-        z_copies(FAR_Z, each)
-
-    sb_copies(lambda copy: copy.start())
+            if k:
+                op(k)
+            else:
+                pl.when(core == 0)(lambda: op(0))
 
     def hd_copy(k):
         to = ring(z, k)
@@ -310,36 +285,7 @@
             partner,
         )
 
-    z_copies(EARLY_Z, lambda k: hd_copy(k).start())
-
-    landed(hw, load_sem.at[4])
-
-    def hot_chunk(c, total):
-        cols = pl.ds(pl.multiple_of(c * CHUNK, CHUNK), CHUNK)
-        normed = (tok[:, cols].astype(F32) * scale * gain[:, cols]).astype(BF16)
-        return total + lax.dot_general(
-            hw[:, cols], normed, (((1,), (1,)), ((), ())), preferred_element_type=F32
-        )
-
-    hot_t = lax.fori_loop(
-        0, features // CHUNK, hot_chunk, jnp.zeros((32, seqs), F32)
-    )
-    hidden_t = silu(hot_t[:16]) * hot_t[16:]
-    hh[core * RING + z] = jnp.concatenate([hidden_t, jnp.zeros_like(hidden_t)], axis=1).astype(
-        BF16
-    )
-
-    def hh_copy(k):
-        return remote(
-            hh.at[core * RING + z],
-            hh.at[core * RING + z],
-            hh_send,
-            hh_recv,
-            along_z(ring(z, k)),
-            partner,
-        )
-
-    z_copies(FAR_Z, lambda k: hh_copy(k).start())
+    z_copies((*NEAR_Z, 0), lambda k: hd_copy(k).start())
 
     half = lax.rem(z, 2)
     rows = lax.div(z, 2)
@@ -382,11 +328,43 @@
         block = cd[pl.ds(slots[k] * LANES, LANES), :]
         cds[k // 2, :, LANES * (k % 2) : LANES * (k % 2) + LANES] = jnp.transpose(block)
 
+    pl.semaphore_wait(zgo, 2)
+    z_copies(BEYOND_Z, lambda k: hd_copy(k).start())
+
+    landed(hw, load_sem.at[4])
+
+    def hot_chunk(c, total):
+        cols = pl.ds(pl.multiple_of(c * CHUNK, CHUNK), CHUNK)
+        normed = (tok[:, cols].astype(F32) * scale * gain[:, cols]).astype(BF16)
+        return total + lax.dot_general(
+            hw[:, cols], normed, (((1,), (1,)), ((), ())), preferred_element_type=F32
+        )
+
+    hot_t = lax.fori_loop(
+        0, features // CHUNK, hot_chunk, jnp.zeros((32, seqs), F32)
+    )
+    hidden_t = silu(hot_t[:16]) * hot_t[16:]
+    hh[core * RING + z] = jnp.concatenate([hidden_t, jnp.zeros_like(hidden_t)], axis=1).astype(
+        BF16
+    )
+
+    def hh_copy(k):
+        return remote(
+            hh.at[core * RING + z],
+            hh.at[core * RING + z],
+            hh_send,
+            hh_recv,
+            along_z(ring(z, k)),
+            partner,
+        )
+
+    z_copies((*FAR_Z, 0), lambda k: hh_copy(k).start())
+
     def cd_copy(k, to):
         return remote(
             cds.at[pair_of(core, to)],
             cdr.at[core, p],
-            cd_send,
+            plane_send,
             cd_recv.at[core],
             in_plane(to),
             partner,
@@ -397,36 +375,14 @@
         def _():
             cd_copy(k, to).start()
 
-    def s2_copies(group, op, own=None):
-        for at in range(Z_FIRST, RING):
-            to = lax.rem(pair_of(group, p) + at, RING)
-            copy = remote(
-                s2.at[group, at - Z_FIRST],
-                r2.at[group * RING + z],
-                s2_send.at[group],
-                r2_recv.at[group],
-                along_z(to),
-                partner,
-            )
-
-            @pl.when(to != z)
-            def _():
-                op(copy)
-
-            if own is not None:
-
-                @pl.when(to == z)
-                def _():
-                    own(at - Z_FIRST)
-
-    def sq_copy(group, b):
-        to = swap(group, pair_at(z, b))
-        return to, remote(
-            sq.at[group, b],
-            r2.at[group * RING + p],
-            sq_send.at[group, b],
+    def s2_copy(group, k):
+        to = ring(z, k)
+        return remote(
+            s2.at[group, to],
+            r2.at[group * RING + z],
+            s2_send,
             r2_recv.at[group],
-            in_plane(jnp.maximum(to, 0)),
+            along_z(to),
             partner,
         )
 
@@ -436,7 +392,7 @@
         return remote(
             h3.at[group, piece],
             h3.at[group, piece],
-            h3_send.at[group],
+            h3_send,
             h3_recv.at[group],
             along_z(ring(z, k)),
             partner,
@@ -456,60 +412,31 @@
     @pl.when(core == 0)
     def _():
         pl.semaphore_wait(go, 1)
-        for k in LATE_Z:
-            hd_copy(k).start()
         plane_copies(FAR_PLANE, start_cd)
 
     @pl.when(adds)
     def _():
-        for group in (1, 0):
-            for b in range(Z_FIRST):
-                pair = pair_at(z, b)
-
-                @pl.when(pair < PAIRS)
-                def _():
-                    if group:
-                        total = s1[jnp.minimum(pair, PAIRS - 1), b].astype(F32)
-                    else:
-                        total = jnp.zeros(s1.shape[2:], F32)
-                    landed(rb.at[group, b, pl.ds(0, RING - group)], sb_recv.at[group, b])
-                    for k in range(group, RING):
-                        total = total + rb[group, b, ring(z, k)].astype(F32)
-                    sq[group, b] = total.astype(BF16)
-                    to, copy = sq_copy(group, b)
-
-                    @pl.when(to != p)
-                    def _():
-                        copy.start()
-
-                    @pl.when(to == p)
-                    def _():
-                        r2[group * RING + p] = sq[group, b]
-
         for group in (1, 0):
 
             @pl.when(works(group))
             def _():
                 if group:
-                    total = s1[pair_of(1, p), Z_FIRST:].astype(F32)
+                    total = s1[pair_of(1, p)].astype(F32)
                 else:
-                    total = jnp.zeros((RING - Z_FIRST, *s1.shape[2:]), F32)
-                landed(r1.at[group, pl.ds(0, RING - group)], s1_recv.at[group])
+                    total = jnp.zeros(s1.shape[1:], F32)
+                base = group * RING
+                landed(r1.at[pl.ds(base, RING - group)], s1_recv.at[group])
                 for k in range(group, RING):
-                    total = total + r1[group, ring(p, k)].astype(F32)
+                    total = total + r1[base + ring(p, k)].astype(F32)
                 s2[group] = total.astype(BF16)
-
-                def own(at):
-                    r2[group * RING + z] = s2[group, at]
-
-                s2_copies(group, lambda copy: copy.start(), own)
+                for k in FAR_Z:
+                    s2_copy(group, k).start()
+                r2[base + z] = s2[group, z]
 
         pl.semaphore_signal(
             go, inc=1, device_id=(hot, x_hi * 2), device_id_type=MESH
         )
 
-        for k in LATE_Z:
-            hd_copy(k).start()
         plane_copies(FAR_PLANE, start_cd)
         cdr[1, p] = cds[pair_of(1, p)]
 
@@ -536,6 +463,8 @@
             down = hdp[:, :, LANES * q : LANES * q + LANES].reshape(2 * LANES, LANES)
             acc[q] = jnp.dot(jnp.transpose(down), hidden, preferred_element_type=F32)
 
+        pl.semaphore_wait(xgo, 1)
+
         def await_pair(group):
             @pl.when(works(group))
             def _():
@@ -595,21 +524,17 @@
     out_ref[16:32, :] = result[:, seqs:].astype(BF16)
 
     fewer = jnp.logical_and(adds, works(1))
-    ends = jnp.logical_or(z == 0, z == RING - 1)
 
     @pl.when(fewer)
     def _():
-        landed(r1.at[0, pl.ds(0, PAIRS - 1)], s1_send)
-        landed(cdr.at[0, pl.ds(0, PAIRS - 1)], cd_send)
+        landed(r1.at[pl.ds(0, 2 * PAIRS - 2)], plane_send)
 
     @pl.when(jnp.logical_not(fewer))
     def _():
-        landed(r1.at[0, pl.ds(0, PAIRS)], s1_send)
-        landed(cdr.at[0, pl.ds(0, PAIRS)], cd_send)
+        landed(r1.at[pl.ds(0, 2 * PAIRS)], plane_send)
 
     @pl.when(core == 0)
     def _():
-        landed(r2.at[pl.ds(0, 14)], sb_send)
         landed(hdp.at[pl.ds(0, RING)], hd_send)
         landed(hh.at[pl.ds(0, RING)], hh_send)
         lv_copy.wait_send()
@@ -618,38 +543,18 @@
     def _():
         landed(hdp.at[pl.ds(0, RING - 1)], hd_send)
         landed(hh.at[pl.ds(0, RING - 1)], hh_send)
-
-        @pl.when(ends)
+        landed(fs.at[pl.ds(0, 4 * RING - 1)], fs_send)
+        both_groups = jnp.logical_and(works(0), works(1))
+
+        @pl.when(both_groups)
         def _():
-            landed(r2.at[pl.ds(0, 13)], sb_send)
-
-        @pl.when(jnp.logical_not(ends))
+            landed(r2.at[pl.ds(0, 2 * RING - 2)], s2_send)
+            landed(hh.at[pl.ds(0, 2 * RING - 2)], h3_send)
+
+        @pl.when(jnp.logical_not(both_groups))
         def _():
-            landed(r2.at[pl.ds(0, 12)], sb_send)
-
-        for group in range(2):
-            z_first = lax.rem(z + RING - pair_of(group, p), RING) < Z_FIRST
-
-            @pl.when(jnp.logical_and(works(group), z_first))
-            def _():
-                landed(r2.at[pl.ds(0, RING - Z_FIRST)], s2_send.at[group])
-
-            @pl.when(jnp.logical_and(works(group), jnp.logical_not(z_first)))
-            def _():
-                landed(r2.at[pl.ds(0, RING - Z_FIRST - 1)], s2_send.at[group])
-
-            @pl.when(works(group))
-            def _():
-                landed(h3.at[group, pl.ds(0, RING - 1)], h3_send.at[group])
-
-            for b in range(Z_FIRST):
-                to, copy = sq_copy(group, b)
-
-                @pl.when(jnp.logical_and(pair_at(z, b) < PAIRS, to != p))
-                def _():
-                    copy.wait_send()
-
-        landed(fs.at[pl.ds(0, 4 * RING - 1)], fs_send)
+            landed(r2.at[pl.ds(0, RING - 1)], s2_send)
+            landed(hh.at[pl.ds(0, RING - 1)], h3_send)
 
 
 def on_device(
@@ -682,10 +587,8 @@
             pltpu.VMEM(block_mask.shape[::-1], jnp.int32),
             pltpu.VMEM((32, LANES), jnp.int32),
             pltpu.VMEM((PAIRS, RING, 2, 16, LANES), BF16),
-            pltpu.VMEM((2, RING, RING - Z_FIRST, 2, 16, LANES), BF16),
-            pltpu.VMEM((2, Z_FIRST, RING, 2, 16, LANES), BF16),
-            pltpu.VMEM((2, Z_FIRST, 2, 16, LANES), BF16),
-            pltpu.VMEM((2, RING - Z_FIRST, 2, 16, LANES), BF16),
+            pltpu.VMEM((2 * RING, RING, 2, 16, LANES), BF16),
+            pltpu.VMEM((2, RING, 2, 16, LANES), BF16),
             pltpu.VMEM((2 * RING, 2, 16, LANES), BF16),
             pltpu.VMEM((2, RING, 16, LANES), BF16),
             pltpu.VMEM((PAIRS, LANES, 2 * LANES), BF16),
@@ -700,20 +603,18 @@
             dma,
             dma((2,)),
             dma,
-            dma((2, Z_FIRST)),
-            dma((2, Z_FIRST)),
+            dma((2,)),
+            dma,
             dma((2,)),
             dma((2,)),
-            dma((2,)),
-            dma((2,)),
-            dma,
-            dma((2,)),
-            dma,
-            dma,
-            dma,
-            dma,
-            dma,
-            dma,
+            dma,
+            dma,
+            dma,
+            dma,
+            dma,
+            dma,
+            pltpu.SemaphoreType.REGULAR,
+            pltpu.SemaphoreType.REGULAR,
             pltpu.SemaphoreType.REGULAR,
             dma,
             dma,

time: 32.1 us -> 31.6 us (0.984)
  Pallas kernels: 31.4 us -> 30.8 us
    pallas_call x1, Pallas kernels: 31.4 us -> 30.8 us  [on_device(): pl.pallas_call(kernel, out_shape=jax.ShapeDtypeStruct((32, seqs), BF16),...]
where the time goes in v5:
time: 31.6 us; the launch traced here: 31.4 us
  Pallas kernels  30.8 us (97%)
  local copies, waits for them, and re-layouts  0.6 us (2%)
    pallas_call x1, Pallas kernels, on_device(): pl.pallas_call(kernel, out_shape=jax.ShapeDtypeStruct((32, seqs), BF16),...  30.8 us

profile of v5, /device:TPU:1, one launch (start us, length us, event | category | flops | bytes accessed | tf_op | source)
XLA Modules:
  0.0 31.4 jit_solution(538203351365341273)
XLA Ops:
  0.0 30.8 %shard_map.100 = bf16[32,64]{1,0:T(8,128)(2,1)S(1)} custom-call(bf16[64,8192]{1,0:T(8,128)(2,1)} %tok_hbm.1, f32[1,8192]{1,0:T(1,128)} %bitcast.5, bf16[16,8192]{1,0:T(8,128)(2,1)} %hg_hbm.1, bf16[16,8192]{1,0:T(8,128)(2,1)} %hu_hbm.1, bf16[16,8192]{1,0:T(8,128)(2,1)} %hd_hbm.1, s32[1,4096]{1,0:T(1,128)} %bitcast.6, bf16[128,3584]{1,0:T(8,128)(2,1)} %cg_hbm.1, ...), custom_call_target="tpu_custom_call" | custom-call | tf_op jit(solution)/shard_map/pallas_call | solution.py:575
  30.8 0.6 %copy.12 = bf16[64,32]{0,1:T(8,128)(2,1)} copy(bf16[64,32]{0,1:T(8,128)(2,1)S(1)} %bitcast.4) | data formatting | bytes 8192

commit v6 on v5

--- a/solution.py
+++ b/solution.py
@@ -143,8 +143,12 @@
         (hidx_hbm, hidx, 5),
         (cd_hbm, cd, 6),
     ]
-    for src, dst, sem in loads:
-        pltpu.make_async_copy(src, dst, load_sem.at[sem]).start()
+
+    def start_loads(some):
+        for src, dst, sem in some:
+            pltpu.make_async_copy(src, dst, load_sem.at[sem]).start()
+
+    start_loads(loads[:5])
 
     def columns_of(zz):
         return pl.ds(pl.multiple_of(zz * RING * LANES, RING * LANES), RING * LANES)
@@ -152,10 +156,6 @@
     own_piece = pltpu.make_async_copy(
         hd_hbm.at[:, columns_of(z)], hdp.at[RING + z], load_sem.at[7]
     )
-
-    @pl.when(adds)
-    def _():
-        own_piece.start()
 
     barrier = pltpu.get_barrier_semaphore()
 
@@ -187,11 +187,7 @@
     mpad[0:blocks_here, 0:seqs] = msk[...]
     block_id = lax.broadcasted_iota(jnp.int32, mpad.shape, 0)
     lane_id = lax.broadcasted_iota(jnp.int32, mpad.shape, 1)
-    active = mpad[...]
-    step = 1
-    while step < LANES:
-        active = jnp.maximum(active, pltpu.roll(active, step, 1))
-        step *= 2
+    active = jnp.broadcast_to(jnp.max(mpad[...], axis=1, keepdims=True), mpad.shape)
     upto = active
     step = 1
     while step < 32:
@@ -210,12 +206,18 @@
         return total + x * x
 
     squares = lax.fori_loop(
-        0, features // LANES, add_squares, jnp.zeros((seqs, LANES), F32), unroll=8
+        0, features // LANES, add_squares, jnp.zeros((seqs, LANES), F32), unroll=32
     )
     scale = lax.rsqrt(jnp.sum(squares, axis=1, keepdims=True) / features + EPS)
     mine = (tok[:, place(hot)].astype(F32) * scale * gain[:, place(hot)]).astype(BF16)
 
     landed(cgu, load_sem.at[3])
+    start_loads(loads[5:])
+
+    @pl.when(adds)
+    def _():
+        own_piece.start()
+
     for k in range(CAP):
         cols = pl.ds(slots[k] * LANES, LANES)
         both = jnp.concatenate([cgu[0, :, cols], cgu[1, :, cols]], axis=1)
@@ -398,15 +400,17 @@
             partner,
         )
 
-    def fs_copy(k, other, core_to):
-        cold_to = lax.rem(x_hi + other, 2) * 2 + core_to
+    def fs_copy(to, x_to, core_to):
+        dy = lax.rem(to // 2 + 4 - lax.div(p, 2), 4)
+        dx = lax.rem(to + p, 2)
+        dc = lax.rem(x_to + x_hi, 2)
         return remote(
-            fs.at[4 * k + cold_to],
-            fr.at[2 * k + other],
+            fs.at[4 * to + 2 * x_to + core_to],
+            fr.at[2 * (2 * dy + dx) + dc],
             fs_send,
             fs_recv,
-            in_plane(in_plane_at(k)[0]),
-            cold_to,
+            in_plane(to),
+            2 * x_to + core_to,
         )
 
     @pl.when(core == 0)
@@ -496,17 +500,21 @@
         await_pair(0)
 
         values = pair_hidden(0)
-        terms = [pair_term(0, values, in_plane_at(k)[0]) for k in (*FAR_PLANE, 0)]
-        for k, term in zip((*FAR_PLANE, 0), terms):
+        terms = [pair_term(0, values, to) for to in range(RING)]
+        for to, term in enumerate(terms):
             for c in range(4):
-                fs[4 * k + c] = jnp.concatenate(
+                fs[4 * to + c] = jnp.concatenate(
                     [term[32 * c : 32 * c + 16], term[32 * c + 16 : 32 * c + 32]], axis=1
                 ).astype(BF16)
-            for other, core_to in ((1, 0), (1, 1), (0, 0), (0, 1)):
-                if k + other or not core_to:
-                    fs_copy(k, other, core_to).start()
-
-        fr[0] = fs[cold]
+            for x_to, core_to in ((0, 1), (0, 0), (1, 1), (1, 0)):
+                copy = fs_copy(to, x_to, core_to)
+                if core_to:
+                    own = jnp.logical_and(to == p, x_hi == x_to)
+                    pl.when(jnp.logical_not(own))(copy.start)
+                else:
+                    copy.start()
+
+        fr[0] = fs[4 * p + cold]
 
     @pl.when(adds)
     def _():

time: 31.6 us -> 31.1 us (0.984)
  Pallas kernels: 30.8 us -> 30.3 us
    pallas_call x1, Pallas kernels: 30.8 us -> 30.3 us  [on_device(): pl.pallas_call(kernel, out_shape=jax.ShapeDtypeStruct((32, seqs), BF16),...]
where the time goes in v6:
time: 31.1 us; the launch traced here: 30.9 us
  Pallas kernels  30.3 us (97%)
  local copies, waits for them, and re-layouts  0.6 us (2%)
    pallas_call x1, Pallas kernels, on_device(): pl.pallas_call(kernel, out_shape=jax.ShapeDtypeStruct((32, seqs), BF16),...  30.3 us

profile of v6, /device:TPU:1, one launch (start us, length us, event | category | flops | bytes accessed | tf_op | source)
XLA Modules:
  0.0 30.9 jit_solution(2729444512551278705)
XLA Ops:
  0.0 30.3 %shard_map.100 = bf16[32,64]{1,0:T(8,128)(2,1)S(1)} custom-call(bf16[64,8192]{1,0:T(8,128)(2,1)} %tok_hbm.1, f32[1,8192]{1,0:T(1,128)} %bitcast.5, bf16[16,8192]{1,0:T(8,128)(2,1)} %hg_hbm.1, bf16[16,8192]{1,0:T(8,128)(2,1)} %hu_hbm.1, bf16[16,8192]{1,0:T(8,128)(2,1)} %hd_hbm.1, s32[1,4096]{1,0:T(1,128)} %bitcast.6, bf16[128,3584]{1,0:T(8,128)(2,1)} %cg_hbm.1, ...), custom_call_target="tpu_custom_call" | custom-call | tf_op jit(solution)/shard_map/pallas_call | solution.py:583
  30.3 0.6 %copy.12 = bf16[64,32]{0,1:T(8,128)(2,1)} copy(bf16[64,32]{0,1:T(8,128)(2,1)S(1)} %bitcast.4) | data formatting | bytes 8192

commit v7 on v6

--- a/solution.py
+++ b/solution.py
@@ -390,13 +390,13 @@
 
     piece = half * 4 + rows
 
-    def h3_copy(group, k):
+    def h3_copy(group, to):
         return remote(
             h3.at[group, piece],
             h3.at[group, piece],
             h3_send,
             h3_recv.at[group],
-            along_z(ring(z, k)),
+            along_z(to),
             partner,
         )
 
@@ -456,8 +456,8 @@
                     both = both + pieces[i].astype(F32)
                 live = lv[group].astype(F32)
                 h3[group, piece] = (silu(both[0]) * both[1] * live).astype(BF16)
-                for k in FAR_Z:
-                    h3_copy(group, k).start()
+                for to in range(RING):
+                    pl.when(to != z)(h3_copy(group, to).start)
 
         own_piece.wait()
         landed(hdp.at[pl.ds(0, 2 * RING - 1)], hd_recv)

time: 31.1 us -> 31.1 us (level)
  no operation moved by 1% of the time
where the time goes in v7:
time: 31.1 us; the launch traced here: 30.9 us
  Pallas kernels  30.3 us (97%)
  local copies, waits for them, and re-layouts  0.6 us (2%)
    pallas_call x1, Pallas kernels, on_device(): pl.pallas_call(kernel, out_shape=jax.ShapeDtypeStruct((32, seqs), BF16),...  30.3 us

profile of v7, /device:TPU:1, one launch (start us, length us, event | category | flops | bytes accessed | tf_op | source)
XLA Modules:
  0.0 30.9 jit_solution(13235073844044843233)
XLA Ops:
  0.0 30.3 %shard_map.100 = bf16[32,64]{1,0:T(8,128)(2,1)S(1)} custom-call(bf16[64,8192]{1,0:T(8,128)(2,1)} %tok_hbm.1, f32[1,8192]{1,0:T(1,128)} %bitcast.5, bf16[16,8192]{1,0:T(8,128)(2,1)} %hg_hbm.1, bf16[16,8192]{1,0:T(8,128)(2,1)} %hu_hbm.1, bf16[16,8192]{1,0:T(8,128)(2,1)} %hd_hbm.1, s32[1,4096]{1,0:T(1,128)} %bitcast.6, bf16[128,3584]{1,0:T(8,128)(2,1)} %cg_hbm.1, ...), custom_call_target="tpu_custom_call" | custom-call | tf_op jit(solution)/shard_map/pallas_call | solution.py:583
  30.3 0.6 %copy.12 = bf16[64,32]{0,1:T(8,128)(2,1)} copy(bf16[64,32]{0,1:T(8,128)(2,1)S(1)} %bitcast.4) | data formatting | bytes 8192
